TPU v7x, 256 devices: a whole 4x4x8 slice. The times are simulated.
256 devices in a mesh: blk: 256 (over z, y, x, core).
Axes of the slice: x: 4, y: 4, z: 8, core: 2. Of those that a mesh axis runs over, the one named last changes fastest.
Arguments:
- populations: float32 [1024, 27, 4096], P('blk'), may hold values from 0.6 to 1.4
- scalars: float32 [1024, 9, 4096], P('blk'), may hold values from 0 to 1
- coarse_old: float32 [1024, 27, 512], P('blk'), may hold values from 0.6 to 1.4
- coarse_new: float32 [1024, 27, 512], P('blk'), may hold values from 0.6 to 1.4
- levels: int32 [1024], replicated, may hold values 0 or 1
- neighbours: int32 [1024, 6], P('blk'), may hold values from 0 to 1023, as said below
- relax_rates: float32 [27], replicated, may hold values from 0.5 to 1.9
- diffusivity: float32 [9], replicated, may hold values from 0.02 to 0.15
- stoichiometry: float32 [9], replicated, may hold values from -1 to 1
Outputs:
- new_populations: float32 [1024, 27, 4096], P('blk')
- new_scalars: float32 [1024, 9, 4096], P('blk')
- coarse_return: float32 [1024, 3456], P('blk')
Inputs may be any that keep to these rules, and one draw needn't show every extreme that they name: `neighbours`: block k lies in slot k % 4 of device k // 4. The blocks 4 * 2 * L up to 4 * 2 * (L + 1) - 1 form layer L (0 <= L < 128), held by devices 2 L and 2 L + 1; the blocks beside a block of layer L on sides 0 to 3 lie in layer L, the one on side 4 in layer L - 1 and the one on side 5 in layer L + 1, taken modulo 128. The relation is symmetric: if m is beside k on side q, k is beside m on side q xor 1. Hence the device of every listed block is at most 3 devices from the device of block k, counting cyclically over all devices.
All inputs are finite; a program needn't handle non-finite values.
Results may differ from a plain program's by a relative error of at most 0.0001.
Values sent between devices are 32-bit elements; how exact they have to be, the bound alone decides.
No kernel may reach another device: no remote copies, remote signals or barrier semaphores. Data moves between devices by JAX's collectives and lax.ppermute only.
A program may use at most 128 MiB of HBM per device.

v0:
```python
import jax
import jax.numpy as jnp
import numpy as np
from jax import lax
from jax.experimental import pallas as pl
from jax.experimental.pallas import tpu as pltpu
from jax.sharding import PartitionSpec as P

F32 = jnp.float32
VEL = [(a, b, c) for a in (-1, 0, 1) for b in (-1, 0, 1) for c in (-1, 0, 1)]
ROWS, LANES = 32, 128
CHUNK = 8


def shape_of(*dims):
    return jax.ShapeDtypeStruct(dims, F32)


def iota(rows, axis):
    return lax.broadcasted_iota(jnp.int32, (rows, LANES), axis)


def chunk_at(v):
    return pl.ds(pl.multiple_of(v * CHUNK, CHUNK), CHUNK)


def roll_lanes(x, by):
    if isinstance(by, int):
        by = by % LANES
        if by == 0:
            return x
    return pltpu.roll(x, by, 1)


def forward_moments(values):
    out = list(values)
    for stride in (9, 3, 1):
        for i in range(27):
            if (i // stride) % 3 == 0:
                low, mid, high = out[i], out[i + stride], out[i + 2 * stride]
                both = low + high
                out[i] = both + 4.0 * mid
                out[i + stride] = high - low
                out[i + 2 * stride] = both
    return out


def plus(x, y):
    if x is None:
        return y
    return x if y is None else x + y


def minus(x, y):
    if y is None:
        return x
    return -y if x is None else x - y


def backward_moments(values):
    out = list(values)
    for stride in (9, 3, 1):
        for i in range(27):
            if (i // stride) % 3 == 0:
                m0, m1, m2 = out[i], out[i + stride], out[i + 2 * stride]
                out[i] = minus(m2, m1)
                out[i + stride] = minus(m0, m2)
                out[i + 2 * stride] = plus(m1, m2)
    return out


def collide(g, rate):
    m = forward_moments(g)
    rho = m[0]
    j = (m[9], m[3], m[1])
    square = [x * x * (1.0 / 72.0) for x in j]
    relaxed = [None] * 27
    for k in range(27):
        digits = (k // 9, (k // 3) % 3, k % 3)
        odd = [d for d in range(3) if digits[d] == 1]
        twos = [d for d in range(3) if digits[d] == 2]
        if k in (0, 9, 3, 1):
            continue
        if not odd:
            level = rho
            for d in twos:
                level = level + square[d]
        elif len(odd) == 1:
            level = j[odd[0]]
        elif len(odd) == 2:
            level = j[odd[0]] * j[odd[1]] * (1.0 / 216.0)
        else:
            level = None
        if level is not None and twos:
            level = level * (3.0 ** -len(twos))
        relaxed[k] = minus(m[k], level) * (rate(k) * (1.0 / 64.0))
    back = backward_moments(relaxed)
    post = []
    for i, c in enumerate(VEL):
        factor = 2.0 ** sum(abs(x) for x in c)
        post.append(g[i] - (back[i] if factor == 1.0 else factor * back[i]))
    return post, j


def grow_index():
    r, l = iota(CHUNK, 0), iota(CHUNK, 1)
    return (r // 4) % 2 * 64 + r % 2 * 32 + l // 32 * 8 + l % 16 // 2


def grow_row(row, index):
    return jnp.take_along_axis(jnp.broadcast_to(row, (CHUNK, LANES)), index, axis=1)


PER_BLOCK = 36
FIELDS = 4 * PER_BLOCK + 1


def fetch(sources, targets, sems, first=0):
    copies = [pltpu.make_async_copy(a, b, sems.at[first + i]) for i, (a, b) in enumerate(zip(sources, targets))]
    for copy in copies:
        copy.start()

    def ready():
        for copy in copies:
            copy.wait()

    return ready


def begin_kernel(
    info_in, levels_in, near_in, rates_in, pop, scal, old, new, out, up, down,
    pops, scals, olds, news, info, levels, near, rates, sems,
):
    ready = fetch((info_in, levels_in, near_in, rates_in), (info, levels, near, rates), sems, 7)
    copies = []
    for v in range(4):
        rows = pl.ds(32 * v, 32)
        copies.append(pltpu.make_async_copy(pop.at[:, rows, :], pops.at[:, rows, :], sems.at[v]))
    copies.append(pltpu.make_async_copy(old, olds, sems.at[4]))
    copies.append(pltpu.make_async_copy(new, news, sems.at[5]))
    copies.append(pltpu.make_async_copy(scal, scals, sems.at[6]))
    for copy in copies:
        copy.start()
    index = grow_index()
    ready()
    layer, core = info[0], info[1]
    row, lane = iota(CHUNK, 0), iota(CHUNK, 1)
    meta = jnp.zeros((CHUNK, LANES), F32)
    for b in range(4):
        for q in range(6):
            here = jnp.logical_and(row == b, lane == q + 8)
            meta = jnp.where(here, near[b, q].astype(F32), meta)
    out[FIELDS - 1, 0:8, :] = meta

    def fine_of(b):
        return levels[layer * 8 + core * 4 + b] == 1

    for v in range(4):
        copies[v].wait()

        @pl.loop(0, 4)
        def _(b):
            @pl.when(fine_of(b))
            def _():
                at = pl.ds(8 * v, 8)
                from_rows = pl.ds(32 * v + b, 8, stride=4)
                post, _j = collide([pops[p, from_rows, :] for p in range(27)], lambda k: rates[k])
                for p in range(27):
                    out[b * PER_BLOCK + p, at, :] = post[p]

    for copy in copies[4:]:
        copy.wait()

    @pl.loop(0, 4)
    def _(b):
        @pl.when(fine_of(b))
        def _():
            for m in range(9):
                for v in range(4):
                    out[b * PER_BLOCK + 27 + m, pl.ds(8 * v, 8), :] = scals[m, pl.ds(32 * v + b, 8, stride=4), :]

        @pl.when(jnp.logical_not(fine_of(b)))
        def _():
            for p in range(27):
                for v in range(4):
                    before = olds[p, pl.ds(4 * v + b, 1), :]
                    after = news[p, pl.ds(4 * v + b, 1), :]
                    out[b * PER_BLOCK + 27 + p // 8, pl.ds(p % 8 * 4 + v, 1), :] = 0.5 * (before + after)
                    out[b * PER_BLOCK + p, pl.ds(8 * v, 8), :] = grow_row(before, index)


    pack_faces(out, up, down, meta)


def pack_faces(out, up, down, meta=None):
    lane = iota(CHUNK, 1) % 16

    @pl.loop(0, 4)
    def _(v):
        at = chunk_at(v)
        for ref, digit, start in ((up, 2, 15), (down, 0, 0)):
            for b in range(4):
                fields = [out[b * PER_BLOCK + 3 * e + digit, at, :] for e in range(9)]
                fields += [out[b * PER_BLOCK + 27 + e, at, :] for e in range(7)]
                ref[b, at, :] = pack_into(fields, 0, start, lane)
            rest = pack_into([out[b * PER_BLOCK + 34 + e, at, :] for b in range(4) for e in range(2)], 0, start, lane)
            ref[4, at, :] = rest if meta is None else jnp.where(lane < 8, rest, meta)


def spot(block, core):
    return (block % 8) ^ (core * 4)


def y_up(own, beside, even, group):
    turned = jnp.where(even, pltpu.roll(beside, CHUNK - 1, 0), pltpu.roll(own, 1, 0))
    return roll_lanes(jnp.where(group < 7, own, turned), 16)


def y_down(own, beside, even, group):
    turned = jnp.where(even, pltpu.roll(own, CHUNK - 1, 0), pltpu.roll(beside, 1, 0))
    return roll_lanes(jnp.where(group > 0, own, turned), -16)


def chunks(ref, *lead):
    return [ref[(*lead, pl.ds(8 * v, 8), slice(None))] for v in range(4)]


def x_up(own, beyond, row):
    turned = [pltpu.roll(x, 2, 0) for x in own]
    before = [beyond] + turned[:3]
    return [jnp.where(row < 2, a, b) for a, b in zip(before, turned)]


def x_down(own, beyond, row):
    turned = [pltpu.roll(x, CHUNK - 2, 0) for x in own]
    after = turned[1:] + [beyond]
    return [jnp.where(row >= 6, a, b) for a, b in zip(after, turned)]


def put(ref, lead, values):
    for v in range(4):
        ref[(*lead, pl.ds(8 * v, 8), slice(None))] = values[v]


def sections_xy(refs, faces, mid, dest, info, levels, near, ready):
    row = iota(CHUNK, 0)
    even = row % 2 == 0
    group = iota(CHUNK, 1) // 16

    for half, ref in enumerate(refs):

        @pl.loop(0, 4)
        def _(i):
            for p, c in enumerate(VEL):
                if c[0] == 1:
                    faces[half * 4 + i, p] = pltpu.roll(ref[i * PER_BLOCK + p, pl.ds(24, 8), :], 2, 0)
                elif c[0] == -1:
                    faces[half * 4 + i, p] = pltpu.roll(ref[i * PER_BLOCK + p, pl.ds(0, 8), :], CHUNK - 2, 0)

    ready()
    core = info[1]
    fine_of = fine_in(info, levels)

    for half, ref in enumerate(refs):

        @pl.loop(0, 4)
        def _(i):
            b = half * 4 + i
            fine = fine_of(b)
            fields = [p for p in range(27) if half == 0 or VEL[p][1] != 0]

            @pl.when(fine)
            def _():
                low, high = spot(near[b, 0], core), spot(near[b, 1], core)
                for p in fields:
                    values = chunks(ref, i * PER_BLOCK + p)
                    if VEL[p][0] == 1:
                        values = x_up(values, faces[low, p], row)
                    elif VEL[p][0] == -1:
                        values = x_down(values, faces[high, p], row)
                    put(mid, (b, p), values)

            @pl.when(jnp.logical_not(fine))
            def _():
                for p in fields:
                    if VEL[p][1] != 0:
                        put(mid, (b, p), chunks(ref, i * PER_BLOCK + p))

    @pl.loop(0, 4)
    def _(b):
        @pl.when(fine_of(b))
        def _():
            low, high = spot(near[b, 2], core), spot(near[b, 3], core)
            for p, c in enumerate(VEL):
                for v in range(4):
                    at = pl.ds(8 * v, 8)
                    value = mid[b, p, at, :]
                    if c[1] == 1:
                        value = y_up(value, mid[low, p, at, :], even, group)
                    elif c[1] == -1:
                        value = y_down(value, mid[high, p, at, :], even, group)
                    dest[b, p, at, :] = value


def pack_into(fields, first_slot, start, lane):
    out = None
    for e, field in enumerate(fields):
        slot = first_slot + e
        moved = roll_lanes(field, slot - start)
        out = moved if out is None else jnp.where(lane == slot, moved, out)
    return out


def fine_in(info, levels):
    return lambda b: levels[info[0] * 8 + spot(b, info[1])] == 1


def plane_kernel(
    info_in, levels_in, diffusivity_in, stoichiometry_in, own, other, dest, table, parts,
    mid, faces, old, info, levels, near, diffusivity, stoichiometry, sems,
):
    row = iota(CHUNK, 0)
    both = jnp.where(row < 4, own[FIELDS - 1, 0:8, :], pltpu.roll(other[FIELDS - 1, 0:8, :], 4, 0))
    table[...] = roll_lanes(both, -8).astype(jnp.int32)
    ready = fetch(
        (info_in, levels_in, table, diffusivity_in, stoichiometry_in), (info, levels, near, diffusivity, stoichiometry), sems
    )
    gather_species((own, other), old)
    sections_xy((own, other), faces, mid, dest, info, levels, near, ready)
    species_begin(old, parts, info, levels, near, diffusivity, stoichiometry)


def settle(incoming, raw):
    for way in range(2):
        for half in range(2):
            for i in range(4):
                put(raw, (way, half * 4 + i), chunks(incoming[way][half], i))


def arrive(info, levels, table, core, raw, mid, done):
    row, slot = iota(CHUNK, 0), iota(CHUNK, 1) % 16
    even, group = row % 2 == 0, iota(CHUNK, 1) // 16
    x_plus, x_minus = jnp.logical_and(slot >= 6, slot < 9), slot < 3
    y_plus = jnp.logical_and(slot < 9, slot % 3 == 2)
    y_minus = jnp.logical_and(slot < 9, slot % 3 == 0)
    blocks = [(way, b) for way in range(2) for b in range(8)]
    fine = [levels[info[2 + way] * 8 + spot(b, core)] == 1 for way, b in blocks]

    def beside(way, b, q):
        return spot(table[b, 16 * way + 8 + q], core)

    for (way, b), flag in zip(blocks, fine):
        own = chunks(raw, way, b)
        before = x_up(own, pltpu.roll(raw[way, beside(way, b, 0), pl.ds(24, 8), :], 2, 0), row)
        after = x_down(own, pltpu.roll(raw[way, beside(way, b, 1), pl.ds(0, 8), :], CHUNK - 2, 0), row)
        to_plus, to_minus = jnp.logical_and(x_plus, flag), jnp.logical_and(x_minus, flag)
        put(mid, (way, b), [jnp.where(to_plus, x, jnp.where(to_minus, y, z)) for x, y, z in zip(before, after, own)])
    for (way, b), flag in zip(blocks, fine):
        low, high = beside(way, b, 2), beside(way, b, 3)
        to_plus, to_minus = jnp.logical_and(y_plus, flag), jnp.logical_and(y_minus, flag)
        for v in range(4):
            at = pl.ds(8 * v, 8)
            here = mid[way, b, at, :]
            before = y_up(here, mid[way, low, at, :], even, group)
            after = y_down(here, mid[way, high, at, :], even, group)
            done[way, b, at, :] = jnp.where(to_plus, before, jnp.where(to_minus, after, here))


def face_reader(done, rest, below, above):
    def faces(m, at):
        if m < 7:
            slot = 9 + m
            return roll_lanes(done[0, below, at, :], -slot), roll_lanes(done[1, above, at, :], 15 - slot)
        low = LANES - 2 * (below % 4) - (m - 7)
        high = (LANES + 15 - 2 * (above % 4) - (m - 7)) % LANES
        return pltpu.roll(rest[0, below // 4, at, :], low, 1), pltpu.roll(rest[1, above // 4, at, :], high, 1)

    return faces


def z_section(h, up, down, depth):
    g = []
    for p, c in enumerate(VEL):
        e = p // 3
        value = h(p)
        if c[2] == 1:
            value = jnp.where(depth == 0, roll_lanes(up, -e), roll_lanes(value, 1))
        elif c[2] == -1:
            value = jnp.where(depth == 15, roll_lanes(down, 15 - e), roll_lanes(value, -1))
        g.append(value)
    return g


def gather_species(halves, old):
    for half, ref_in in enumerate(halves):

        @pl.loop(0, 4)
        def _(i):
            for m in range(9):
                put(old, (half * 4 + i, m), chunks(ref_in, i * PER_BLOCK + 27 + m))


def species_begin(y_ref, parts, info, levels, near, diffusivity, stoichiometry):
    row, lanes = iota(CHUNK, 0), iota(CHUNK, 1)
    even = row % 2 == 0
    group, depth = lanes // 16, lanes % 16
    fine_of = fine_in(info, levels)

    @pl.loop(0, 4)
    def _(b):
        @pl.when(fine_of(b))
        def _():
            def gone(edge, q):
                return jnp.logical_and(edge, levels[near[b, q]] != 1)

            lost = [
                gone(row < 2, 0), gone(row >= 6, 1),
                gone(jnp.logical_and(even, group == 0), 2),
                gone(jnp.logical_and(jnp.logical_not(even), group == 7), 3),
            ]
            sides = [spot(near[b, q], info[1]) for q in range(4)]
            burning = [
                x * y * jnp.exp(4.0 * (t - 1.0))
                for x, y, t in zip(chunks(y_ref, b, 0), chunks(y_ref, b, 1), chunks(y_ref, b, 8))
            ]
            for m in range(9):
                y = chunks(y_ref, b, m)
                low_x = pltpu.roll(y_ref[sides[0], m, pl.ds(24, 8), :], 2, 0)
                high_x = pltpu.roll(y_ref[sides[1], m, pl.ds(0, 8), :], CHUNK - 2, 0)
                lower_x, upper_x = x_up(y, low_x, row), x_down(y, high_x, row)
                lower_x[0] = jnp.where(lost[0], y[0], lower_x[0])
                upper_x[3] = jnp.where(lost[1], y[3], upper_x[3])
                for v in range(4):
                    at = pl.ds(8 * v, 8)
                    here = y[v]
                    pairs = [
                        (lower_x[v], upper_x[v]),
                        (
                            jnp.where(lost[2], here, y_up(here, y_ref[sides[2], m, at, :], even, group)),
                            jnp.where(lost[3], here, y_down(here, y_ref[sides[3], m, at, :], even, group)),
                        ),
                        (
                            jnp.where(depth == 0, here, roll_lanes(here, 1)),
                            jnp.where(depth == 15, here, roll_lanes(here, -1)),
                        ),
                    ]
                    spread = None
                    for d, (lower, upper) in enumerate(pairs):
                        parts[b * PER_BLOCK + 9 + 9 * d + m, at, :] = upper - lower
                        both = upper + lower
                        spread = both if spread is None else spread + both
                    parts[b * PER_BLOCK + m, at, :] = (
                        here + diffusivity[m] * (spread - 6.0 * here) + stoichiometry[m] * burning[v]
                    )


def species_end(parts, b, y_of, faces, flux, flags, diffusivity, store):
    depth = iota(CHUNK, 1) % 16
    at_low = jnp.logical_and(depth == 0, flags[0] == 1)
    at_high = jnp.logical_and(depth == 15, flags[1] == 1)
    for v in range(4):
        at = pl.ds(8 * v, 8)
        flow = [flux[d, at, :] for d in range(3)]
        for m in range(9):
            here = y_of(m, at)
            low, high = faces(m, at)
            low = jnp.where(at_low, low - here, 0.0)
            high = jnp.where(at_high, high - here, 0.0)
            base, along_x, along_y, along_z = (parts[b * PER_BLOCK + 9 * kind + m, at, :] for kind in range(4))
            drift = flow[0] * along_x + flow[1] * along_y + flow[2] * (along_z + (high - low))
            store(m, v, base - drift + diffusivity[m] * (low + high))


WIDE = 640


def reduce_tables():
    l = np.arange(LANES)[:, None]
    c = np.arange(WIDE)[None, :]
    e, cell = c // 64, c % 64
    live = c < 576
    along_x = (l // 32 * 8 + l % 16 // 2 == cell % 32) & live
    along_y = [(l // 16 + 8 * a == e) & (l % 16 // 2 == cell % 8) & live for a in range(2)]
    along_z = (l % 16 == e) & (l // 32 == cell % 4) & live
    side = np.concatenate([along_x, along_y[0], along_y[1]], axis=0)
    return jnp.asarray(side, jnp.bfloat16), jnp.asarray(along_z, jnp.bfloat16)


def wide_iota(axis):
    return lax.broadcasted_iota(jnp.int32, (ROWS, WIDE), axis)


def times(x, w):
    total = None
    for _ in range(3):
        part = x.astype(jnp.bfloat16)
        x = x - part.astype(F32)
        product = jnp.dot(part, w, preferred_element_type=F32)
        total = product if total is None else total + product
    return total


def column_sums(spread, k, keep):
    return jnp.sum(jnp.where(keep, spread[pl.ds(k * ROWS, ROWS), :], 0.0), axis=0, keepdims=True)


def put_pair(out, s, base, first, second):
    moved = pltpu.roll(second, 64, 1)
    out[pl.ds(s, 1), pl.ds(base, 512)] = first[:, 0:512]
    out[pl.ds(s, 1), pl.ds(base + 512, 128)] = first[:, 512:640] + moved[:, 0:128]
    out[pl.ds(s, 1), pl.ds(base + 640, 512)] = moved[:, 128:640]


def middle_kernel(
    info_in, levels_in, near_in, rates_in, diffusivity_in, own, held, parts, up_own, up_other, down_own, down_other,
    out, up, down, table,
    raw, mid, done, rest, flux,
    info, levels, near, rates, diffusivity, far, sems,
):
    index = grow_index()
    incoming = ((up_own, up_other), (down_own, down_other))
    row, lane = iota(CHUNK, 0), iota(CHUNK, 1)
    below, above = [
        jnp.where(row < 4, one[4, pl.ds(0, 8), :], pltpu.roll(two[4, pl.ds(0, 8), :], 4, 0)) for one, two in incoming
    ]
    table[...] = jnp.where(lane < 16, below, roll_lanes(above, 16)).astype(jnp.int32)
    ready = fetch(
        (info_in, levels_in, near_in, rates_in, diffusivity_in, table),
        (info, levels, near, rates, diffusivity, far),
        sems,
    )
    settle(incoming, raw)
    for way in range(2):
        for half in range(2):
            put(rest, (way, half), chunks(incoming[way][half], 4))

    ready()
    core = info[1]
    fine_of = fine_in(info, levels)
    arrive(info, levels, far, core, raw, mid, done)

    @pl.loop(0, 4)
    def _(b):
        @pl.when(fine_of(b))
        def _():
            below, above = spot(near[b, 4], core), spot(near[b, 5], core)

            @pl.loop(0, 4)
            def _(v):
                at = chunk_at(v)
                g = z_section(lambda p: held[b, p, at, :], done[0, below, at, :], done[1, above, at, :], depth_of())
                post, j = collide(g, lambda k: rates[k])
                for p in range(27):
                    out[b * PER_BLOCK + p, at, :] = post[p]
                for d in range(3):
                    flux[d, at, :] = j[d] * (0.5 / 216.0)

            def store(m, v, value):
                out[b * PER_BLOCK + 27 + m, pl.ds(8 * v, 8), :] = value

            species_end(
                parts, b, lambda m, at: own[b * PER_BLOCK + 27 + m, at, :], face_reader(done, rest, below, above), flux,
                [levels[near[b, q]] for q in (4, 5)], diffusivity, store,
            )

        @pl.when(jnp.logical_not(fine_of(b)))
        def _():
            for p in range(27):
                for v in range(4):
                    line = own[b * PER_BLOCK + 27 + p // 8, pl.ds(p % 8 * 4 + v, 1), :]
                    out[b * PER_BLOCK + p, pl.ds(8 * v, 8), :] = grow_row(line, index)
            for m in range(9):
                put(out, (b * PER_BLOCK + 27 + m,), [jnp.zeros((CHUNK, LANES), F32)] * 4)

    pack_faces(out, up, down)


def depth_of():
    return iota(CHUNK, 1) % 16


def second_plane_kernel(
    info_in, levels_in, near_in, diffusivity_in, stoichiometry_in, own, other, own_before, other_before, tables,
    dest, sides_out, parts,
    mid, faces, old, edge_x, edge_y, needed, picked_x, picked_y, spread,
    info, levels, near, diffusivity, stoichiometry, sems,
):
    ready = fetch(
        (info_in, levels_in, near_in, diffusivity_in, stoichiometry_in), (info, levels, near, diffusivity, stoichiometry), sems
    )
    gather_species((own, other), old)
    sections_xy((own, other), faces, mid, dest, info, levels, near, ready)
    species_begin(old, parts, info, levels, near, diffusivity, stoichiometry)
    core = info[1]
    fine_of = fine_in(info, levels)
    for b in range(8):
        needed[b] = 0
    for s in range(4):
        for q in range(4):

            @pl.when(jnp.logical_not(fine_of(s)))
            def _(s=s, q=q):
                needed[spot(near[s, q], core)] = 1

    group, odd = iota(CHUNK, 1) // 16, iota(CHUNK, 0) % 2 == 1
    for half, (one, two) in enumerate(((own_before, own), (other_before, other))):

        @pl.loop(0, 4)
        def _(i):
            b = half * 4 + i

            def total(p, at):
                return one[i * PER_BLOCK + p, at, :] + two[i * PER_BLOCK + p, at, :]

            @pl.when(jnp.logical_and(fine_of(b), needed[b] == 1))
            def _():
                for side in range(2):
                    at = pl.ds(30, 2) if side == 0 else pl.ds(0, 2)
                    for e in range(9):
                        edge_x[b, side, pl.ds(2 * e, 2), :] = total(18 + e if side == 0 else e, at)
                    edge_x[b, side, pl.ds(18, 14), :] = jnp.zeros((14, LANES), F32)
                for v in range(4):
                    at = pl.ds(8 * v, 8)
                    packs = [None, None]
                    for e in range(9):
                        p_low = 9 * (e // 3) + e % 3
                        slot = e % 8
                        high = roll_lanes(total(p_low + 6, at), 16 * (slot - 7))
                        both = jnp.where(odd, high, roll_lanes(total(p_low, at), 16 * slot))
                        held_pack = packs[e // 8]
                        packs[e // 8] = both if held_pack is None else jnp.where(group == slot, both, held_pack)
                    for a in range(2):
                        edge_y[b, a, at, :] = packs[a]

    row, col = wide_iota(0), wide_iota(1)
    e_of, cell = col // 64, col % 64
    keep_x = jnp.logical_and(row // 2 == e_of, row % 2 == cell // 32)
    keep_y = row // 4 == cell // 8
    odd_row = row % 2 == 1
    any_coarse = jnp.logical_not(jnp.logical_and(jnp.logical_and(fine_of(0), fine_of(1)), jnp.logical_and(fine_of(2), fine_of(3))))
    sides_out[...] = jnp.zeros((4, 2304), F32)

    @pl.when(any_coarse)
    def _():
        for q in range(4):
            for s in range(4):
                live = jnp.logical_and(jnp.logical_not(fine_of(s)), levels[near[s, q]] == 1)
                m = spot(near[s, q], core)
                rows = pl.ds((q % 2 * 4 + s) * ROWS, ROWS)
                if q < 2:
                    picked_x[rows, :] = jnp.where(live, 0.125 * edge_x[m, q], 0.0)
                else:
                    for a in range(2):
                        picked_y[rows, pl.ds(a * LANES, LANES)] = jnp.where(live, 0.125 * edge_y[m, a], 0.0)
        for pair, picked, weights in ((0, picked_x, tables[0:128, :]), (1, picked_y, tables[128:384, :])):
            spread[...] = times(picked[...], weights)
            for s in range(4):
                keeps = (keep_x, keep_x)
                if pair:
                    keeps = (jnp.logical_and(keep_y, odd_row), jnp.logical_and(keep_y, jnp.logical_not(odd_row)))
                put_pair(
                    sides_out, s, pair * 1152,
                    column_sums(spread, s, keeps[0]), column_sums(spread, 4 + s, keeps[1]),
                )


def end_kernel(
    info_in, levels_in, near_in, far_in, diffusivity_in, held, own, parts,
    up_own, up_other, down_own, down_other, up_own_before, up_other_before, down_own_before, down_other_before,
    sides, weights, pop, scal,
    pop_out, scal_out, returned_out,
    raw, mid, done, rest, before, pops, scals, returned, flux, picked, spread,
    info, levels, near, far, diffusivity, sems,
):
    ready = fetch(
        (info_in, levels_in, near_in, far_in, diffusivity_in), (info, levels, near, far, diffusivity), sems, 6
    )
    incoming = ((up_own, up_other), (down_own, down_other))
    for way in range(2):
        for half in range(2):
            put(rest, (way, half), chunks(incoming[way][half], 4))
    settle(((up_own_before, up_other_before), (down_own_before, down_other_before)), before)
    settle(incoming, raw)
    ready()
    core = info[1]
    fine_of = fine_in(info, levels)
    arrive(info, levels, far, core, raw, mid, done)
    depth = iota(CHUNK, 1) % 16
    row, col = wide_iota(0), wide_iota(1)
    keep = row // 4 * 2 + row % 2 == col % 64 // 4
    copies = []
    for v in range(4):
        at = pl.ds(8 * v, 8)

        @pl.loop(0, 4)
        def _(s):
            rows = pl.ds(32 * v + s, 8, stride=4)

            @pl.when(fine_of(s))
            def _():
                below, above = spot(near[s, 4], core), spot(near[s, 5], core)
                g = z_section(lambda p: held[s, p, at, :], done[0, below, at, :], done[1, above, at, :], depth)
                for p in range(27):
                    pops[p, rows, :] = g[p]
                m = forward_moments(g)
                for d, i in enumerate((9, 3, 1)):
                    flux[s, d, at, :] = m[i] * (0.5 / 216.0)

            @pl.when(jnp.logical_not(fine_of(s)))
            def _():
                for p in range(27):
                    pops[p, rows, :] = pop[p, rows, :]

        rows = pl.ds(32 * v, 32)
        copies.append(pltpu.make_async_copy(pops.at[:, rows, :], pop_out.at[:, rows, :], sems.at[v]))
        copies[-1].start()

    returned[:, 0:2304] = sides[...]
    returned[:, 2304:3456] = jnp.zeros((4, 1152), F32)
    any_coarse = jnp.logical_not(jnp.logical_and(jnp.logical_and(fine_of(0), fine_of(1)), jnp.logical_and(fine_of(2), fine_of(3))))

    @pl.when(any_coarse)
    def _():
        for way in range(2):
            for s in range(4):
                m = spot(near[s, 4 + way], core)
                live = jnp.logical_and(jnp.logical_not(fine_of(s)), levels[near[s, 4 + way]] == 1)
                face = jnp.where(live, 0.125 * (before[way, m] + raw[way, m]), 0.0)
                picked[pl.ds((way * 4 + s) * ROWS, ROWS), :] = face
        spread[...] = times(picked[...], weights[...])
        for s in range(4):
            put_pair(returned, s, 2304, column_sums(spread, s, keep), column_sums(spread, 4 + s, keep))

    copies.append(pltpu.make_async_copy(returned, returned_out, sems.at[5]))
    copies[-1].start()

    @pl.loop(0, 4)
    def _(s):
        @pl.when(fine_of(s))
        def _():
            def store(m, v, value):
                scals[m, pl.ds(32 * v + s, 8, stride=4), :] = value

            species_end(
                parts, s, lambda m, at: own[s * PER_BLOCK + 27 + m, at, :],
                face_reader(done, rest, spot(near[s, 4], core), spot(near[s, 5], core)), flux.at[s],
                [levels[near[s, q]] for q in (4, 5)], diffusivity, store,
            )

        @pl.when(jnp.logical_not(fine_of(s)))
        def _():
            for v in range(4):
                at = pl.ds(32 * v + s, 8, stride=4)
                for m in range(9):
                    scals[m, at, :] = scal[m, at, :]

    copies.append(pltpu.make_async_copy(scals, scal_out, sems.at[4]))
    copies[-1].start()
    for copy in copies:
        copy.wait()


def specs(kinds):
    table = {
        "s": pl.BlockSpec(memory_space=pltpu.SMEM),
        "v": pl.BlockSpec(memory_space=pltpu.VMEM),
        "h": pl.BlockSpec(memory_space=pltpu.HBM),
        "a": pl.BlockSpec(memory_space=pl.ANY),
    }
    return [table[kind] for kind in kinds]


def call(kernel, kinds, outs, out_kinds, scratch, name, megabytes, flops):
    return pl.pallas_call(
        kernel,
        in_specs=specs(kinds),
        out_specs=specs(out_kinds),
        out_shape=outs,
        scratch_shapes=scratch,
        name=name,
        compiler_params=pltpu.CompilerParams(vmem_limit_bytes=megabytes << 20),
        cost_estimate=pl.CostEstimate(flops=flops, transcendentals=0, bytes_accessed=8 << 20),
    )


def interleave(x):
    blocks, n, cells = x.shape
    x = x.reshape(blocks, n, cells // LANES, LANES)
    return jnp.transpose(x, (1, 2, 0, 3)).reshape(n, cells // LANES * blocks, LANES)


def separate(x):
    n, rows, _ = x.shape
    x = jnp.transpose(x.reshape(n, rows // 4, 4, LANES), (2, 0, 1, 3))
    return x.reshape(4, n, rows // 4 * LANES)


def local(
    populations, scalars, coarse_old, coarse_new, levels, neighbours, relax_rates, diffusivity, stoichiometry
):
    devices = lax.axis_size("blk")
    me = lax.axis_index("blk")
    layer, layers = me // 2, devices // 2
    info = jnp.stack([layer, me % 2, (layer + layers - 1) % layers, (layer + 1) % layers]).astype(jnp.int32)
    swap = [(i, i ^ 1) for i in range(devices)]
    rise = [(i, (i + 2) % devices) for i in range(devices)]
    fall = [(i, (i - 2) % devices) for i in range(devices)]

    def move(x, pairs):
        return lax.ppermute(x, "blk", pairs)

    def vmem(*lead):
        return pltpu.VMEM((*lead, ROWS, LANES), F32)

    full = (ROWS, LANES)
    pop, scal = interleave(populations), interleave(scalars)
    old, new = interleave(coarse_old), interleave(coarse_new)
    side_table, z_table = reduce_tables()
    fields = FIELDS - 1
    semaphores = pltpu.SemaphoreType.DMA
    own, up, down = call(
        begin_kernel,
        "ahhhhhhh",
        [shape_of(FIELDS, *full), shape_of(5, *full), shape_of(5, *full)],
        "vvv",
        [pltpu.VMEM(x.shape, F32) for x in (pop, scal, old, new)]
        + [pltpu.SMEM(x.shape, x.dtype) for x in (info, levels, neighbours, relax_rates)]
        + [semaphores((11,))],
        "begin",
        12,
        1 << 27,
    )(info, *[pltpu.with_memory_space_constraint(x, pltpu.HBM) for x in (levels, neighbours, relax_rates, pop, scal, old, new)])
    other = move(own, swap)
    up, down = move(up, rise), move(down, fall)
    face = pltpu.VMEM((8, 27, CHUNK, LANES), F32)
    table_shape = jax.ShapeDtypeStruct((CHUNK, LANES), jnp.int32)

    def smem(*arrays):
        return [pltpu.SMEM(x.shape, x.dtype) for x in arrays]

    held, near, parts = call(
        plane_kernel,
        "aaaavv",
        [shape_of(4, 27, *full), table_shape, shape_of(4 * PER_BLOCK, *full)],
        "vvv",
        [vmem(8, 27), face, vmem(8, 9)]
        + smem(info, levels, table_shape, diffusivity, stoichiometry) + [semaphores((5,))],
        "plane",
        12,
        1 << 27,
    )(info, levels, diffusivity, stoichiometry, own, other)
    held, up, down = lax.optimization_barrier((held, up, down))
    arrived = (up, move(up, swap), down, move(down, swap))
    landing = [vmem(2, 8), vmem(2, 8), vmem(2, 8), vmem(2, 2)]
    own_next, up_next, down_next, table = call(
        middle_kernel,
        "aaaaavvvvvvv",
        [shape_of(fields, *full), shape_of(5, *full), shape_of(5, *full), table_shape],
        "vvvv",
        landing
        + [vmem(3)]
        + smem(info, levels, table_shape, relax_rates, diffusivity, table_shape)
        + [semaphores((6,))],
        "middle",
        14,
        1 << 28,
    )(
        info, levels, near, relax_rates, diffusivity, own, held, parts, *arrived
    )
    other_next = move(own_next, swap)
    up, down = move(up_next, rise), move(down_next, fall)
    held, sides, parts = call(
        second_plane_kernel,
        "aaaaavvvvv",
        [shape_of(4, 27, *full), shape_of(4, 2304), shape_of(4 * PER_BLOCK, *full)],
        "vvv",
        [vmem(8, 27), face, vmem(8, 9), vmem(8, 2), vmem(8, 2), pltpu.SMEM((8,), jnp.int32)]
        + [pltpu.VMEM((8 * ROWS, LANES), F32), pltpu.VMEM((8 * ROWS, 2 * LANES), F32), pltpu.VMEM((8 * ROWS, WIDE), F32)]
        + smem(info, levels, table_shape, diffusivity, stoichiometry) + [semaphores((5,))],
        "plane2",
        14,
        1 << 27,
    )(info, levels, near, diffusivity, stoichiometry, own_next, other_next, own, other, side_table)
    held, sides, up, down = lax.optimization_barrier((held, sides, up, down))
    pop_out, scal_out, returned = call(
        end_kernel,
        "aaaaa" + "v" * 15,
        [shape_of(27, 128, LANES), shape_of(9, 128, LANES), shape_of(4, 3456)],
        "hhh",
        landing
        + [vmem(2, 8), pltpu.VMEM(pop.shape, F32), pltpu.VMEM(scal.shape, F32)]
        + [pltpu.VMEM((4, 3456), F32), vmem(4, 3)]
        + [pltpu.VMEM((8 * ROWS, LANES), F32), pltpu.VMEM((8 * ROWS, WIDE), F32)]
        + smem(info, levels, table_shape, table_shape, diffusivity) + [semaphores((11,))],
        "end",
        16,
        1 << 27,
    )(
        info, levels, near, table, diffusivity, held, own_next, parts,
        up, move(up, swap), down, move(down, swap), *arrived, sides, z_table, pop, scal,
    )
    return separate(pop_out), separate(scal_out), returned


def solution(mesh):
    in_specs = (
        P("blk", None, None), P("blk", None, None), P("blk", None, None), P("blk", None, None),
        P(), P("blk", None), P(), P(), P(),
    )
    out_specs = (P("blk", None, None), P("blk", None, None), P("blk", None))
    return jax.shard_map(local, mesh=mesh, in_specs=in_specs, out_specs=out_specs, check_vma=False)
```

profile of v0, /device:TPU:1, one launch (start us, length us, event | category | flops | bytes accessed | tf_op | source)
XLA Modules:
  0.0 43.1 jit_solution(2422254627562406088)
XLA Ops:
  0.6 0.0 copy-start.4
  0.6 0.0 copy-start.5
  0.7 0.0 copy-start.7
  0.7 0.1 pad_add_fusion.info_in
  0.8 3.1 %begin.1 = (f32[145,32,128]{2,1,0:T(8,128)S(1)}, f32[5,32,128]{2,1,0:T(8,128)S(1)}, f32[5,32,128]{2,1,0:T(8,128)S(1)}) custom-call(s32[4]{0:T(128)S(1)} %pad_add_fusion.info_in, s32[1024]{0:T(1024)} %levels_in.9, s32[4,6]{1,0:T(4,128)} %near_in.1, f32[27]{0:T(128)} %rates_in.3, f32[27,128,128]{2,1,0:T(8,128)} %bitcast.34, f32[9,128,128]{2,1,0:T(8,128)} %bitcast.36, ...), custom_call_target="tpu_custom_call" | custom-call | flops 134217728 | bytes 8388608 | tf_op jit(solution)/shard_map/begin/pallas_call | solution.py:821
  3.9 3.3 %collective-permute-start = (f32[145,32,128]{2,1,0:T(8,128)S(1)}, f32[145,32,128]{2,1,0:T(8,128)S(1)}, u32[]{:S(2)}, u32[]{:S(2)}) collective-permute-start(f32[145,32,128]{2,1,0:T(8,128)S(1)} %get-tuple-element.26.own.own_before), channel_id=1, source_target_pairs={{0,1},{1,0},{2,3},{3,2},{4,5},{5,4},{6,7},{7,6},{8,9},{9,8},{10,11... | collective-permute-start | bytes 7127048 | tf_op jit(solution)/shard_map/ppermute | solution.py:810
  7.2 0.0 collective-permute-start.1
  7.2 8.5 %collective-permute-start.2 = (f32[5,32,128]{2,1,0:T(8,128)S(1)}, f32[5,32,128]{2,1,0:T(8,128)S(1)}, u32[]{:S(2)}, u32[]{:S(2)}) collective-permute-start(f32[5,32,128]{2,1,0:T(8,128)S(1)} %get-tuple-element.30), channel_id=1, source_target_pairs={{0,254},{1,255},{2,0},{3,1},{4,2},{5,3},{6,4},{7,5},{8,6},{9,7},{1... | collective-permute-start | bytes 245768 | tf_op jit(solution)/shard_map/ppermute | solution.py:810
  15.8 0.0 collective-permute-done.other.other_before
  15.8 2.4 %plane.1 = (f32[4,27,32,128]{3,2,1,0:T(8,128)S(1)}, s32[8,128]{1,0:T(8,128)S(1)}, f32[144,32,128]{2,1,0:T(8,128)S(1)}) custom-call(s32[4]{0:T(128)S(1)} %pad_add_fusion.info_in, s32[1024]{0:T(1024)S(1)} %copy-done.4, f32[9]{0:T(128)S(1)} %copy-done.5, f32[9]{0:T(128)S(1)} %copy-done.7, f32[145,32,128]{2,1,0:T(8,128)S(1)} %get-tuple-element.26.own.own_before, ...), custom_call_target="tpu_custom_call" | custom-call | flops 134217728 | bytes 8388608 | tf_op jit(solution)/shard_map/plane/pallas_call | solution.py:841
  18.2 0.3 collective-permute-done.1.up_own.up_own_before
  18.5 0.0 collective-permute-done.2.down_own.down_own_before
  18.5 0.7 %collective-permute-start.3 = (f32[5,32,128]{2,1,0:T(8,128)S(1)}, f32[5,32,128]{2,1,0:T(8,128)S(1)}, u32[]{:S(2)}, u32[]{:S(2)}) collective-permute-start(f32[5,32,128]{2,1,0:T(8,128)S(1)} %collective-permute-done.1.up_own.up_own_before), channel_id=1, source_target_pairs={{0,1},{1,0},{2,3},{3,2},{4,5},{5,4},{6,7},{7,6},{8,9},{9,8},{10,11... | collective-permute-start | bytes 245768 | tf_op jit(solution)/shard_map/ppermute | solution.py:810
  19.2 0.0 collective-permute-start.4
  19.2 0.9 %collective-permute-done.3.up_other.up_other_before = f32[5,32,128]{2,1,0:T(8,128)S(1)} collective-permute-done((f32[5,32,128]{2,1,0:T(8,128)S(1)}, f32[5,32,128]{2,1,0:T(8,128)S(1)}, u32[]{:S(2)}, u32[]{:S(2)}) %collective-permute-start.3) | collective-permute-done | bytes 81952 | tf_op jit(solution)/shard_map/ppermute | solution.py:810
  20.1 0.4 collective-permute-done.4.down_other.down_other_before
  20.4 4.6 %middle.1 = (f32[144,32,128]{2,1,0:T(8,128)S(1)}, f32[5,32,128]{2,1,0:T(8,128)S(1)}, f32[5,32,128]{2,1,0:T(8,128)S(1)}, s32[8,128]{1,0:T(8,128)S(1)}) custom-call(s32[4]{0:T(128)S(1)} %pad_add_fusion.info_in, s32[1024]{0:T(1024)S(1)} %copy-done.4, s32[8,128]{1,0:T(8,128)S(1)} %get-tuple-element.27.near_in, f32[27]{0:T(128)S(1)} %copy-done.6, ...), custom_call_target="tpu_custom_call" | custom-call | flops 268435456 | bytes 8388608 | tf_op jit(solution)/shard_map/middle/pallas_call | solution.py:855
  25.0 0.1 collective-permute-start.5
  25.1 0.1 collective-permute-start.6
  25.2 0.0 copy-start
  25.2 0.0 copy-start.1
  25.2 0.0 copy-start.3
  25.2 7.0 %collective-permute-start.7 = (f32[5,32,128]{2,1,0:T(8,128)S(1)}, f32[5,32,128]{2,1,0:T(8,128)S(1)}, u32[]{:S(2)}, u32[]{:S(2)}) collective-permute-start(f32[5,32,128]{2,1,0:T(8,128)S(1)} %get-tuple-element.40), channel_id=1, source_target_pairs={{0,254},{1,255},{2,0},{3,1},{4,2},{5,3},{6,4},{7,5},{8,6},{9,7},{1... | collective-permute-start | bytes 245768 | tf_op jit(solution)/shard_map/ppermute | solution.py:810
  32.2 0.0 collective-permute-done.5.other
  32.2 3.7 %plane2.1 = (f32[4,27,32,128]{3,2,1,0:T(8,128)S(1)}, f32[4,2304]{1,0:T(4,128)S(1)}, f32[144,32,128]{2,1,0:T(8,128)S(1)}) custom-call(s32[4]{0:T(128)S(1)} %pad_add_fusion.info_in, s32[1024]{0:T(1024)S(1)} %copy-done.4, s32[8,128]{1,0:T(8,128)S(1)} %get-tuple-element.27.near_in, f32[9]{0:T(128)S(1)} %copy-done.5, f32[9]{0:T(128)S(1)} %copy-done.7, ...), custom_call_target="tpu_custom_call" | custom-call | flops 134217728 | bytes 8388608 | tf_op jit(solution)/shard_map/plane2/pallas_call | solution.py:872
  35.9 0.0 collective-permute-done.6.up_own
  35.9 0.0 collective-permute-done.7.down_own
  35.9 1.0 %collective-permute-start.8 = (f32[5,32,128]{2,1,0:T(8,128)S(1)}, f32[5,32,128]{2,1,0:T(8,128)S(1)}, u32[]{:S(2)}, u32[]{:S(2)}) collective-permute-start(f32[5,32,128]{2,1,0:T(8,128)S(1)} %collective-permute-done.6.up_own), channel_id=1, source_target_pairs={{0,1},{1,0},{2,3},{3,2},{4,5},{5,4},{6,7},{7,6},{8,9},{9,8},{10,11... | collective-permute-start | bytes 245768 | tf_op jit(solution)/shard_map/ppermute | solution.py:810
  36.9 0.1 collective-permute-start.9
  37.0 0.8 %collective-permute-done.8.up_other = f32[5,32,128]{2,1,0:T(8,128)S(1)} collective-permute-done((f32[5,32,128]{2,1,0:T(8,128)S(1)}, f32[5,32,128]{2,1,0:T(8,128)S(1)}, u32[]{:S(2)}, u32[]{:S(2)}) %collective-permute-start.8) | collective-permute-done | bytes 81952 | tf_op jit(solution)/shard_map/ppermute | solution.py:810
  37.8 0.4 collective-permute-done.9.down_other
  38.2 5.0 %end.1 = (f32[27,128,128]{2,1,0:T(8,128)}, f32[9,128,128]{2,1,0:T(8,128)}, f32[4,3456]{1,0:T(4,128)}) custom-call(s32[4]{0:T(128)S(1)} %pad_add_fusion.info_in, s32[1024]{0:T(1024)S(1)} %copy-done.4, s32[8,128]{1,0:T(8,128)S(1)} %get-tuple-element.27.near_in, s32[8,128]{1,0:T(8,128)S(1)} %get-tuple-element.35.far_in, f32[9]{0:T(128)S(1)} %copy-done.5, ...), custom_call_target="tpu_custom_call" | custom-call | flops 134217728 | bytes 8388608 | tf_op jit(solution)/shard_map/end/pallas_call | solution.py:885
  (10 shorter events, 0.0 us)
Async XLA Ops:
  0.6 15.1 %copy-start.4 = (s32[1024]{0:T(1024)S(1)}, s32[1024]{0:T(1024)}, u32[]{:S(2)}) copy-start(s32[1024]{0:T(1024)} %levels_in.9) | copy-start | bytes 12292
  0.6 15.1 %copy-start.5 = (f32[9]{0:T(128)S(1)}, f32[9]{0:T(128)}, u32[]{:S(2)}) copy-start(f32[9]{0:T(128)} %diffusivity_in.7) | copy-start | bytes 112
  0.7 15.1 %copy-start.7 = (f32[9]{0:T(128)S(1)}, f32[9]{0:T(128)}, u32[]{:S(2)}) copy-start(f32[9]{0:T(128)} %stoichiometry_in.3) | copy-start | bytes 112
  3.9 11.8 %collective-permute-start = (f32[145,32,128]{2,1,0:T(8,128)S(1)}, f32[145,32,128]{2,1,0:T(8,128)S(1)}, u32[]{:S(2)}, u32[]{:S(2)}) collective-permute-start(f32[145,32,128]{2,1,0:T(8,128)S(1)} %get-tuple-element.26.own.own_before), channel_id=1, source_target_pairs={{0,1},{1,0},{2,3},{3,2},{4,5},{5,4},{6,7},{7,6},{8,9},{9,8},{10,11... | collective-permute-start | bytes 7127048 | tf_op jit(solution)/shard_map/ppermute | solution.py:810
  7.2 11.2 %collective-permute-start.1 = (f32[5,32,128]{2,1,0:T(8,128)S(1)}, f32[5,32,128]{2,1,0:T(8,128)S(1)}, u32[]{:S(2)}, u32[]{:S(2)}) collective-permute-start(f32[5,32,128]{2,1,0:T(8,128)S(1)} %get-tuple-element.29), channel_id=1, source_target_pairs={{0,2},{1,3},{2,4},{3,5},{4,6},{5,7},{6,8},{7,9},{8,10},{9,11},{10,... | collective-permute-start | bytes 245768 | tf_op jit(solution)/shard_map/ppermute | solution.py:810
  7.2 13.2 %copy-start.6 = (f32[27]{0:T(128)S(1)}, f32[27]{0:T(128)}, u32[]{:S(2)}) copy-start(f32[27]{0:T(128)} %rates_in.3) | copy-start | bytes 328
  7.2 11.2 %collective-permute-start.2 = (f32[5,32,128]{2,1,0:T(8,128)S(1)}, f32[5,32,128]{2,1,0:T(8,128)S(1)}, u32[]{:S(2)}, u32[]{:S(2)}) collective-permute-start(f32[5,32,128]{2,1,0:T(8,128)S(1)} %get-tuple-element.30), channel_id=1, source_target_pairs={{0,254},{1,255},{2,0},{3,1},{4,2},{5,3},{6,4},{7,5},{8,6},{9,7},{1... | collective-permute-start | bytes 245768 | tf_op jit(solution)/shard_map/ppermute | solution.py:810
  18.5 1.6 %collective-permute-start.3 = (f32[5,32,128]{2,1,0:T(8,128)S(1)}, f32[5,32,128]{2,1,0:T(8,128)S(1)}, u32[]{:S(2)}, u32[]{:S(2)}) collective-permute-start(f32[5,32,128]{2,1,0:T(8,128)S(1)} %collective-permute-done.1.up_own.up_own_before), channel_id=1, source_target_pairs={{0,1},{1,0},{2,3},{3,2},{4,5},{5,4},{6,7},{7,6},{8,9},{9,8},{10,11... | collective-permute-start | bytes 245768 | tf_op jit(solution)/shard_map/ppermute | solution.py:810
  19.2 1.3 %collective-permute-start.4 = (f32[5,32,128]{2,1,0:T(8,128)S(1)}, f32[5,32,128]{2,1,0:T(8,128)S(1)}, u32[]{:S(2)}, u32[]{:S(2)}) collective-permute-start(f32[5,32,128]{2,1,0:T(8,128)S(1)} %collective-permute-done.2.down_own.down_own_before), channel_id=1, source_target_pairs={{0,1},{1,0},{2,3},{3,2},{4,5},{5,4},{6,7},{7,6},{8,9},{9,8},{10,11... | collective-permute-start | bytes 245768 | tf_op jit(solution)/shard_map/ppermute | solution.py:810
  20.4 11.8 %copy-start.2 = (bf16[384,640]{1,0:T(8,128)(2,1)S(1)}, bf16[384,640]{1,0:T(8,128)(2,1)}, u32[]{:S(2)}) copy-start(bf16[384,640]{1,0:T(8,128)(2,1)} %constant.49.clone.tables) | copy-start | bytes 1474564
  25.0 7.2 %collective-permute-start.5 = (f32[144,32,128]{2,1,0:T(8,128)S(1)}, f32[144,32,128]{2,1,0:T(8,128)S(1)}, u32[]{:S(2)}, u32[]{:S(2)}) collective-permute-start(f32[144,32,128]{2,1,0:T(8,128)S(1)} %get-tuple-element.36.own), channel_id=1, source_target_pairs={{0,1},{1,0},{2,3},{3,2},{4,5},{5,4},{6,7},{7,6},{8,9},{9,8},{10,11... | collective-permute-start | bytes 7077896 | tf_op jit(solution)/shard_map/ppermute | solution.py:810
  25.1 10.8 %collective-permute-start.6 = (f32[5,32,128]{2,1,0:T(8,128)S(1)}, f32[5,32,128]{2,1,0:T(8,128)S(1)}, u32[]{:S(2)}, u32[]{:S(2)}) collective-permute-start(f32[5,32,128]{2,1,0:T(8,128)S(1)} %get-tuple-element.39), channel_id=1, source_target_pairs={{0,2},{1,3},{2,4},{3,5},{4,6},{5,7},{6,8},{7,9},{8,10},{9,11},{10,... | collective-permute-start | bytes 245768 | tf_op jit(solution)/shard_map/ppermute | solution.py:810
  25.2 13.0 %copy-start = (f32[4,27,4096]{2,0,1:T(4,128)S(1)}, f32[4,27,4096]{2,0,1:T(4,128)}, u32[]{:S(2)}) copy-start(f32[4,27,4096]{2,0,1:T(4,128)} %param.11) | copy-start | bytes 5308420
  25.2 12.9 %copy-start.1 = (f32[4,9,4096]{2,0,1:T(4,128)S(1)}, f32[4,9,4096]{2,0,1:T(4,128)}, u32[]{:S(2)}) copy-start(f32[4,9,4096]{2,0,1:T(4,128)} %param.12) | copy-start | bytes 1769476
  25.2 12.9 %copy-start.3 = (bf16[128,640]{1,0:T(8,128)(2,1)S(1)}, bf16[128,640]{1,0:T(8,128)(2,1)}, u32[]{:S(2)}) copy-start(bf16[128,640]{1,0:T(8,128)(2,1)} %constant.50.clone.weights) | copy-start | bytes 491524
  25.2 10.7 %collective-permute-start.7 = (f32[5,32,128]{2,1,0:T(8,128)S(1)}, f32[5,32,128]{2,1,0:T(8,128)S(1)}, u32[]{:S(2)}, u32[]{:S(2)}) collective-permute-start(f32[5,32,128]{2,1,0:T(8,128)S(1)} %get-tuple-element.40), channel_id=1, source_target_pairs={{0,254},{1,255},{2,0},{3,1},{4,2},{5,3},{6,4},{7,5},{8,6},{9,7},{1... | collective-permute-start | bytes 245768 | tf_op jit(solution)/shard_map/ppermute | solution.py:810
  35.9 1.9 %collective-permute-start.8 = (f32[5,32,128]{2,1,0:T(8,128)S(1)}, f32[5,32,128]{2,1,0:T(8,128)S(1)}, u32[]{:S(2)}, u32[]{:S(2)}) collective-permute-start(f32[5,32,128]{2,1,0:T(8,128)S(1)} %collective-permute-done.6.up_own), channel_id=1, source_target_pairs={{0,1},{1,0},{2,3},{3,2},{4,5},{5,4},{6,7},{7,6},{8,9},{9,8},{10,11... | collective-permute-start | bytes 245768 | tf_op jit(solution)/shard_map/ppermute | solution.py:810
  36.9 1.3 %collective-permute-start.9 = (f32[5,32,128]{2,1,0:T(8,128)S(1)}, f32[5,32,128]{2,1,0:T(8,128)S(1)}, u32[]{:S(2)}, u32[]{:S(2)}) collective-permute-start(f32[5,32,128]{2,1,0:T(8,128)S(1)} %collective-permute-done.7.down_own), channel_id=1, source_target_pairs={{0,1},{1,0},{2,3},{3,2},{4,5},{5,4},{6,7},{7,6},{8,9},{9,8},{10,11... | collective-permute-start | bytes 245768 | tf_op jit(solution)/shard_map/ppermute | solution.py:810
where the time goes:
time: 42.9 us; the launch traced here: 43.1 us
  starting transfers between devices  20.7 us (48%)
  Pallas kernels  18.7 us (44%)
  waiting for transfers between devices  2.79 us (7%)
  between operations  0.82 us (2%)
    ppermute x10, starting transfers between devices, move(): return lax.ppermute(x, 'blk', pairs)  20.7 us
    pallas_call x1, Pallas kernels, local(): call(end_kernel, 'aaaaa' + 'v' * 15, [shape_of(27, 128, LANES), shape_of(...  4.97 us
    pallas_call x1, Pallas kernels, local(): call(middle_kernel, 'aaaaavvvvvvv', [shape_of(fields, *full), shape_of(5,...  4.56 us
    pallas_call x1, Pallas kernels, local(): call(second_plane_kernel, 'aaaaavvvvv', [shape_of(4, 27, *full), shape_of...  3.68 us
    pallas_call x1, Pallas kernels, local(): call(begin_kernel, 'ahhhhhhh', [shape_of(FIELDS, *full), shape_of(5, *ful...  3.12 us
    ppermute x10, waiting for transfers between devices, move(): return lax.ppermute(x, 'blk', pairs)  2.79 us
    pallas_call x1, Pallas kernels, local(): call(plane_kernel, 'aaaavv', [shape_of(4, 27, *full), table_shape, shape_...  2.37 us
  transfers between devices with their start and end apart: 10, of which 5 were waited for; matrix products, arithmetic and copies ran while one was open for 0% of the time, Pallas kernels for 14%

commit v1 on v0

--- a/solution.py
+++ b/solution.py
@@ -303,12 +303,14 @@
 
 
 def pack_into(fields, first_slot, start, lane):
-    out = None
-    for e, field in enumerate(fields):
-        slot = first_slot + e
-        moved = roll_lanes(field, slot - start)
-        out = moved if out is None else jnp.where(lane == slot, moved, out)
-    return out
+    parts = [(first_slot + e, roll_lanes(field, first_slot + e - start)) for e, field in enumerate(fields)]
+    while len(parts) > 1:
+        joined = []
+        for k in range(0, len(parts) - 1, 2):
+            slot = parts[k + 1][0]
+            joined.append((parts[k][0], jnp.where(lane < slot, parts[k][1], parts[k + 1][1])))
+        parts = joined + parts[len(parts) - len(parts) % 2:]
+    return parts[0][1]
 
 
 def fine_in(info, levels):
@@ -514,7 +516,7 @@
 def middle_kernel(
     info_in, levels_in, near_in, rates_in, diffusivity_in, own, held, parts, up_own, up_other, down_own, down_other,
     out, up, down, table,
-    raw, mid, done, rest, flux,
+    raw, mid, done, rest, flux, moved,
     info, levels, near, rates, diffusivity, far, sems,
 ):
     index = grow_index()
@@ -545,11 +547,16 @@
         def _():
             below, above = spot(near[b, 4], core), spot(near[b, 5], core)
 
+            for v in range(4):
+                at = pl.ds(8 * v, 8)
+                g = z_section(lambda p: held[b, p, at, :], done[0, below, at, :], done[1, above, at, :], depth_of())
+                for p in range(27):
+                    moved[p, at, :] = g[p]
+
             @pl.loop(0, 4)
             def _(v):
                 at = chunk_at(v)
-                g = z_section(lambda p: held[b, p, at, :], done[0, below, at, :], done[1, above, at, :], depth_of())
-                post, j = collide(g, lambda k: rates[k])
+                post, j = collide([moved[p, at, :] for p in range(27)], lambda k: rates[k])
                 for p in range(27):
                     out[b * PER_BLOCK + p, at, :] = post[p]
                 for d in range(3):
@@ -688,32 +695,53 @@
     depth = iota(CHUNK, 1) % 16
     row, col = wide_iota(0), wide_iota(1)
     keep = row // 4 * 2 + row % 2 == col % 64 // 4
-    copies = []
-    for v in range(4):
-        at = pl.ds(8 * v, 8)
-
-        @pl.loop(0, 4)
-        def _(s):
-            rows = pl.ds(32 * v + s, 8, stride=4)
-
-            @pl.when(fine_of(s))
-            def _():
-                below, above = spot(near[s, 4], core), spot(near[s, 5], core)
+    @pl.loop(0, 4)
+    def _(s):
+        below, above = spot(near[s, 4], core), spot(near[s, 5], core)
+
+        @pl.when(fine_of(s))
+        def _():
+            for v in range(4):
+                at = pl.ds(8 * v, 8)
                 g = z_section(lambda p: held[s, p, at, :], done[0, below, at, :], done[1, above, at, :], depth)
                 for p in range(27):
-                    pops[p, rows, :] = g[p]
+                    pops[p, pl.ds(32 * v + s, 8, stride=4), :] = g[p]
                 m = forward_moments(g)
                 for d, i in enumerate((9, 3, 1)):
                     flux[s, d, at, :] = m[i] * (0.5 / 216.0)
 
-            @pl.when(jnp.logical_not(fine_of(s)))
-            def _():
+        @pl.when(jnp.logical_not(fine_of(s)))
+        def _():
+            for v in range(4):
+                rows = pl.ds(32 * v + s, 8, stride=4)
                 for p in range(27):
                     pops[p, rows, :] = pop[p, rows, :]
 
-        rows = pl.ds(32 * v, 32)
-        copies.append(pltpu.make_async_copy(pops.at[:, rows, :], pop_out.at[:, rows, :], sems.at[v]))
-        copies[-1].start()
+    copies = [pltpu.make_async_copy(pops, pop_out, sems.at[0])]
+    copies[-1].start()
+
+    @pl.loop(0, 4)
+    def _(s):
+        @pl.when(fine_of(s))
+        def _():
+            def store(m, v, value):
+                scals[m, pl.ds(32 * v + s, 8, stride=4), :] = value
+
+            species_end(
+                parts, s, lambda m, at: own[s * PER_BLOCK + 27 + m, at, :],
+                face_reader(done, rest, spot(near[s, 4], core), spot(near[s, 5], core)), flux.at[s],
+                [levels[near[s, q]] for q in (4, 5)], diffusivity, store,
+            )
+
+        @pl.when(jnp.logical_not(fine_of(s)))
+        def _():
+            for v in range(4):
+                at = pl.ds(32 * v + s, 8, stride=4)
+                for m in range(9):
+                    scals[m, at, :] = scal[m, at, :]
+
+    copies.append(pltpu.make_async_copy(scals, scal_out, sems.at[4]))
+    copies[-1].start()
 
     returned[:, 0:2304] = sides[...]
     returned[:, 2304:3456] = jnp.zeros((4, 1152), F32)
@@ -734,28 +762,6 @@
     copies.append(pltpu.make_async_copy(returned, returned_out, sems.at[5]))
     copies[-1].start()
 
-    @pl.loop(0, 4)
-    def _(s):
-        @pl.when(fine_of(s))
-        def _():
-            def store(m, v, value):
-                scals[m, pl.ds(32 * v + s, 8, stride=4), :] = value
-
-            species_end(
-                parts, s, lambda m, at: own[s * PER_BLOCK + 27 + m, at, :],
-                face_reader(done, rest, spot(near[s, 4], core), spot(near[s, 5], core)), flux.at[s],
-                [levels[near[s, q]] for q in (4, 5)], diffusivity, store,
-            )
-
-        @pl.when(jnp.logical_not(fine_of(s)))
-        def _():
-            for v in range(4):
-                at = pl.ds(32 * v + s, 8, stride=4)
-                for m in range(9):
-                    scals[m, at, :] = scal[m, at, :]
-
-    copies.append(pltpu.make_async_copy(scals, scal_out, sems.at[4]))
-    copies[-1].start()
     for copy in copies:
         copy.wait()
 
@@ -858,7 +864,7 @@
         [shape_of(fields, *full), shape_of(5, *full), shape_of(5, *full), table_shape],
         "vvvv",
         landing
-        + [vmem(3)]
+        + [vmem(3), vmem(27)]
         + smem(info, levels, table_shape, relax_rates, diffusivity, table_shape)
         + [semaphores((6,))],
         "middle",

time: 42.9 us -> 41.4 us (0.965)
  Pallas kernels: 18.7 us -> 16.1 us
  starting transfers between devices: 20.7 us -> 21.4 us
    pallas_call x1, Pallas kernels: 4.97 us -> 3.53 us  [local(): call(end_kernel, 'aaaaa' + 'v' * 15, [shape_of(27, 128, LANES), shape_of(...]
    pallas_call x1, Pallas kernels: 4.56 us -> 3.7 us  [local(): call(middle_kernel, 'aaaaavvvvvvv', [shape_of(fields, *full), shape_of(5,...]
    ppermute x10, starting transfers between devices: 20.7 us -> 21.4 us  [move(): return lax.ppermute(x, 'blk', pairs)]
where the time goes in v1:
time: 41.4 us; the launch traced here: 41.5 us
  starting transfers between devices  21.4 us (52%)
  Pallas kernels  16.1 us (39%)
  waiting for transfers between devices  3.17 us (8%)
  between operations  0.79 us (2%)
    ppermute x10, starting transfers between devices, move(): return lax.ppermute(x, 'blk', pairs)  21.4 us
    pallas_call x1, Pallas kernels, local(): call(middle_kernel, 'aaaaavvvvvvv', [shape_of(fields, *full), shape_of(5,...  3.7 us
    pallas_call x1, Pallas kernels, local(): call(second_plane_kernel, 'aaaaavvvvv', [shape_of(4, 27, *full), shape_of...  3.68 us
    pallas_call x1, Pallas kernels, local(): call(end_kernel, 'aaaaa' + 'v' * 15, [shape_of(27, 128, LANES), shape_of(...  3.53 us
    ppermute x10, waiting for transfers between devices, move(): return lax.ppermute(x, 'blk', pairs)  3.17 us
    pallas_call x1, Pallas kernels, local(): call(begin_kernel, 'ahhhhhhh', [shape_of(FIELDS, *full), shape_of(5, *ful...  3.17 us
    pallas_call x1, Pallas kernels, local(): call(plane_kernel, 'aaaavv', [shape_of(4, 27, *full), table_shape, shape_...  1.99 us
  transfers between devices with their start and end apart: 10, of which 5 were waited for; matrix products, arithmetic and copies ran while one was open for 0% of the time, Pallas kernels for 14%

profile of v1, /device:TPU:1, one launch (start us, length us, event | category | flops | bytes accessed | tf_op | source)
XLA Modules:
  0.0 41.5 jit_solution(15850281749547045818)
XLA Ops:
  0.6 0.0 copy-start.4
  0.6 0.0 copy-start.5
  0.7 0.0 copy-start.7
  0.7 0.1 pad_add_fusion.info_in
  0.8 3.2 %begin.1 = (f32[145,32,128]{2,1,0:T(8,128)S(1)}, f32[5,32,128]{2,1,0:T(8,128)S(1)}, f32[5,32,128]{2,1,0:T(8,128)S(1)}) custom-call(s32[4]{0:T(128)S(1)} %pad_add_fusion.info_in, s32[1024]{0:T(1024)} %levels_in.9, s32[4,6]{1,0:T(4,128)} %near_in.1, f32[27]{0:T(128)} %rates_in.3, f32[27,128,128]{2,1,0:T(8,128)} %bitcast.34, f32[9,128,128]{2,1,0:T(8,128)} %bitcast.36, ...), custom_call_target="tpu_custom_call" | custom-call | flops 134217728 | bytes 8388608 | tf_op jit(solution)/shard_map/begin/pallas_call | solution.py:827
  4.0 3.3 %collective-permute-start = (f32[145,32,128]{2,1,0:T(8,128)S(1)}, f32[145,32,128]{2,1,0:T(8,128)S(1)}, u32[]{:S(2)}, u32[]{:S(2)}) collective-permute-start(f32[145,32,128]{2,1,0:T(8,128)S(1)} %get-tuple-element.26.own.own_before), channel_id=1, source_target_pairs={{0,1},{1,0},{2,3},{3,2},{4,5},{5,4},{6,7},{7,6},{8,9},{9,8},{10,11... | collective-permute-start | bytes 7127048 | tf_op jit(solution)/shard_map/ppermute | solution.py:816
  7.2 0.0 collective-permute-start.1
  7.2 8.5 %collective-permute-start.2 = (f32[5,32,128]{2,1,0:T(8,128)S(1)}, f32[5,32,128]{2,1,0:T(8,128)S(1)}, u32[]{:S(2)}, u32[]{:S(2)}) collective-permute-start(f32[5,32,128]{2,1,0:T(8,128)S(1)} %get-tuple-element.30), channel_id=1, source_target_pairs={{0,254},{1,255},{2,0},{3,1},{4,2},{5,3},{6,4},{7,5},{8,6},{9,7},{1... | collective-permute-start | bytes 245768 | tf_op jit(solution)/shard_map/ppermute | solution.py:816
  15.7 0.0 collective-permute-done.other.other_before
  15.7 0.0 copy-done.4
  15.7 0.0 copy-done.5
  15.8 2.0 %plane.1 = (f32[4,27,32,128]{3,2,1,0:T(8,128)S(1)}, s32[8,128]{1,0:T(8,128)S(1)}, f32[144,32,128]{2,1,0:T(8,128)S(1)}) custom-call(s32[4]{0:T(128)S(1)} %pad_add_fusion.info_in, s32[1024]{0:T(1024)S(1)} %copy-done.4, f32[9]{0:T(128)S(1)} %copy-done.5, f32[9]{0:T(128)S(1)} %copy-done.7, f32[145,32,128]{2,1,0:T(8,128)S(1)} %get-tuple-element.26.own.own_before, ...), custom_call_target="tpu_custom_call" | custom-call | flops 134217728 | bytes 8388608 | tf_op jit(solution)/shard_map/plane/pallas_call | solution.py:847
  17.8 0.7 %collective-permute-done.1.up_own.up_own_before = f32[5,32,128]{2,1,0:T(8,128)S(1)} collective-permute-done((f32[5,32,128]{2,1,0:T(8,128)S(1)}, f32[5,32,128]{2,1,0:T(8,128)S(1)}, u32[]{:S(2)}, u32[]{:S(2)}) %collective-permute-start.1) | collective-permute-done | bytes 81952 | tf_op jit(solution)/shard_map/ppermute | solution.py:816
  18.5 0.0 collective-permute-done.2.down_own.down_own_before
  18.5 0.7 %collective-permute-start.3 = (f32[5,32,128]{2,1,0:T(8,128)S(1)}, f32[5,32,128]{2,1,0:T(8,128)S(1)}, u32[]{:S(2)}, u32[]{:S(2)}) collective-permute-start(f32[5,32,128]{2,1,0:T(8,128)S(1)} %collective-permute-done.1.up_own.up_own_before), channel_id=1, source_target_pairs={{0,1},{1,0},{2,3},{3,2},{4,5},{5,4},{6,7},{7,6},{8,9},{9,8},{10,11... | collective-permute-start | bytes 245768 | tf_op jit(solution)/shard_map/ppermute | solution.py:816
  19.1 0.0 collective-permute-start.4
  19.1 0.9 %collective-permute-done.3.up_other.up_other_before = f32[5,32,128]{2,1,0:T(8,128)S(1)} collective-permute-done((f32[5,32,128]{2,1,0:T(8,128)S(1)}, f32[5,32,128]{2,1,0:T(8,128)S(1)}, u32[]{:S(2)}, u32[]{:S(2)}) %collective-permute-start.3) | collective-permute-done | bytes 81952 | tf_op jit(solution)/shard_map/ppermute | solution.py:816
  20.1 0.4 collective-permute-done.4.down_other.down_other_before
  20.4 3.7 %middle.1 = (f32[144,32,128]{2,1,0:T(8,128)S(1)}, f32[5,32,128]{2,1,0:T(8,128)S(1)}, f32[5,32,128]{2,1,0:T(8,128)S(1)}, s32[8,128]{1,0:T(8,128)S(1)}) custom-call(s32[4]{0:T(128)S(1)} %pad_add_fusion.info_in, s32[1024]{0:T(1024)S(1)} %copy-done.4, s32[8,128]{1,0:T(8,128)S(1)} %get-tuple-element.27.near_in, f32[27]{0:T(128)S(1)} %copy-done.6, ...), custom_call_target="tpu_custom_call" | custom-call | flops 268435456 | bytes 8388608 | tf_op jit(solution)/shard_map/middle/pallas_call | solution.py:861
  24.1 0.7 %collective-permute-start.5 = (f32[144,32,128]{2,1,0:T(8,128)S(1)}, f32[144,32,128]{2,1,0:T(8,128)S(1)}, u32[]{:S(2)}, u32[]{:S(2)}) collective-permute-start(f32[144,32,128]{2,1,0:T(8,128)S(1)} %get-tuple-element.36.own), channel_id=1, source_target_pairs={{0,1},{1,0},{2,3},{3,2},{4,5},{5,4},{6,7},{7,6},{8,9},{9,8},{10,11... | collective-permute-start | bytes 7077896 | tf_op jit(solution)/shard_map/ppermute | solution.py:816
  24.8 0.0 collective-permute-start.6
  24.8 7.4 %collective-permute-start.7 = (f32[5,32,128]{2,1,0:T(8,128)S(1)}, f32[5,32,128]{2,1,0:T(8,128)S(1)}, u32[]{:S(2)}, u32[]{:S(2)}) collective-permute-start(f32[5,32,128]{2,1,0:T(8,128)S(1)} %get-tuple-element.40), channel_id=1, source_target_pairs={{0,254},{1,255},{2,0},{3,1},{4,2},{5,3},{6,4},{7,5},{8,6},{9,7},{1... | collective-permute-start | bytes 245768 | tf_op jit(solution)/shard_map/ppermute | solution.py:816
  32.2 0.0 collective-permute-done.5.other
  32.2 3.7 %plane2.1 = (f32[4,27,32,128]{3,2,1,0:T(8,128)S(1)}, f32[4,2304]{1,0:T(4,128)S(1)}, f32[144,32,128]{2,1,0:T(8,128)S(1)}) custom-call(s32[4]{0:T(128)S(1)} %pad_add_fusion.info_in, s32[1024]{0:T(1024)S(1)} %copy-done.4, s32[8,128]{1,0:T(8,128)S(1)} %get-tuple-element.27.near_in, f32[9]{0:T(128)S(1)} %copy-done.5, f32[9]{0:T(128)S(1)} %copy-done.7, ...), custom_call_target="tpu_custom_call" | custom-call | flops 134217728 | bytes 8388608 | tf_op jit(solution)/shard_map/plane2/pallas_call | solution.py:878
  35.9 0.0 collective-permute-done.6.up_own
  35.9 0.0 collective-permute-done.7.down_own
  35.9 0.8 %collective-permute-start.8 = (f32[5,32,128]{2,1,0:T(8,128)S(1)}, f32[5,32,128]{2,1,0:T(8,128)S(1)}, u32[]{:S(2)}, u32[]{:S(2)}) collective-permute-start(f32[5,32,128]{2,1,0:T(8,128)S(1)} %collective-permute-done.6.up_own), channel_id=1, source_target_pairs={{0,1},{1,0},{2,3},{3,2},{4,5},{5,4},{6,7},{7,6},{8,9},{9,8},{10,11... | collective-permute-start | bytes 245768 | tf_op jit(solution)/shard_map/ppermute | solution.py:816
  36.7 0.1 collective-permute-start.9
  36.8 0.8 %collective-permute-done.8.up_other = f32[5,32,128]{2,1,0:T(8,128)S(1)} collective-permute-done((f32[5,32,128]{2,1,0:T(8,128)S(1)}, f32[5,32,128]{2,1,0:T(8,128)S(1)}, u32[]{:S(2)}, u32[]{:S(2)}) %collective-permute-start.8) | collective-permute-done | bytes 81952 | tf_op jit(solution)/shard_map/ppermute | solution.py:816
  37.6 0.4 collective-permute-done.9.down_other
  37.9 0.0 copy-done.1
  38.0 3.5 %end.1 = (f32[27,128,128]{2,1,0:T(8,128)}, f32[9,128,128]{2,1,0:T(8,128)}, f32[4,3456]{1,0:T(4,128)}) custom-call(s32[4]{0:T(128)S(1)} %pad_add_fusion.info_in, s32[1024]{0:T(1024)S(1)} %copy-done.4, s32[8,128]{1,0:T(8,128)S(1)} %get-tuple-element.27.near_in, s32[8,128]{1,0:T(8,128)S(1)} %get-tuple-element.35.far_in, f32[9]{0:T(128)S(1)} %copy-done.5, ...), custom_call_target="tpu_custom_call" | custom-call | flops 134217728 | bytes 8388608 | tf_op jit(solution)/shard_map/end/pallas_call | solution.py:891
  (10 shorter events, 0.0 us)
Async XLA Ops:
  0.6 15.1 %copy-start.4 = (s32[1024]{0:T(1024)S(1)}, s32[1024]{0:T(1024)}, u32[]{:S(2)}) copy-start(s32[1024]{0:T(1024)} %levels_in.9) | copy-start | bytes 12292
  0.6 15.1 %copy-start.5 = (f32[9]{0:T(128)S(1)}, f32[9]{0:T(128)}, u32[]{:S(2)}) copy-start(f32[9]{0:T(128)} %diffusivity_in.7) | copy-start | bytes 112
  0.7 15.1 %copy-start.7 = (f32[9]{0:T(128)S(1)}, f32[9]{0:T(128)}, u32[]{:S(2)}) copy-start(f32[9]{0:T(128)} %stoichiometry_in.3) | copy-start | bytes 112
  4.0 11.8 %collective-permute-start = (f32[145,32,128]{2,1,0:T(8,128)S(1)}, f32[145,32,128]{2,1,0:T(8,128)S(1)}, u32[]{:S(2)}, u32[]{:S(2)}) collective-permute-start(f32[145,32,128]{2,1,0:T(8,128)S(1)} %get-tuple-element.26.own.own_before), channel_id=1, source_target_pairs={{0,1},{1,0},{2,3},{3,2},{4,5},{5,4},{6,7},{7,6},{8,9},{9,8},{10,11... | collective-permute-start | bytes 7127048 | tf_op jit(solution)/shard_map/ppermute | solution.py:816
  7.2 11.2 %collective-permute-start.1 = (f32[5,32,128]{2,1,0:T(8,128)S(1)}, f32[5,32,128]{2,1,0:T(8,128)S(1)}, u32[]{:S(2)}, u32[]{:S(2)}) collective-permute-start(f32[5,32,128]{2,1,0:T(8,128)S(1)} %get-tuple-element.29), channel_id=1, source_target_pairs={{0,2},{1,3},{2,4},{3,5},{4,6},{5,7},{6,8},{7,9},{8,10},{9,11},{10,... | collective-permute-start | bytes 245768 | tf_op jit(solution)/shard_map/ppermute | solution.py:816
  7.2 13.2 %copy-start.6 = (f32[27]{0:T(128)S(1)}, f32[27]{0:T(128)}, u32[]{:S(2)}) copy-start(f32[27]{0:T(128)} %rates_in.3) | copy-start | bytes 328
  7.2 11.2 %collective-permute-start.2 = (f32[5,32,128]{2,1,0:T(8,128)S(1)}, f32[5,32,128]{2,1,0:T(8,128)S(1)}, u32[]{:S(2)}, u32[]{:S(2)}) collective-permute-start(f32[5,32,128]{2,1,0:T(8,128)S(1)} %get-tuple-element.30), channel_id=1, source_target_pairs={{0,254},{1,255},{2,0},{3,1},{4,2},{5,3},{6,4},{7,5},{8,6},{9,7},{1... | collective-permute-start | bytes 245768 | tf_op jit(solution)/shard_map/ppermute | solution.py:816
  18.5 1.6 %collective-permute-start.3 = (f32[5,32,128]{2,1,0:T(8,128)S(1)}, f32[5,32,128]{2,1,0:T(8,128)S(1)}, u32[]{:S(2)}, u32[]{:S(2)}) collective-permute-start(f32[5,32,128]{2,1,0:T(8,128)S(1)} %collective-permute-done.1.up_own.up_own_before), channel_id=1, source_target_pairs={{0,1},{1,0},{2,3},{3,2},{4,5},{5,4},{6,7},{7,6},{8,9},{9,8},{10,11... | collective-permute-start | bytes 245768 | tf_op jit(solution)/shard_map/ppermute | solution.py:816
  19.1 1.3 %collective-permute-start.4 = (f32[5,32,128]{2,1,0:T(8,128)S(1)}, f32[5,32,128]{2,1,0:T(8,128)S(1)}, u32[]{:S(2)}, u32[]{:S(2)}) collective-permute-start(f32[5,32,128]{2,1,0:T(8,128)S(1)} %collective-permute-done.2.down_own.down_own_before), channel_id=1, source_target_pairs={{0,1},{1,0},{2,3},{3,2},{4,5},{5,4},{6,7},{7,6},{8,9},{9,8},{10,11... | collective-permute-start | bytes 245768 | tf_op jit(solution)/shard_map/ppermute | solution.py:816
  20.4 11.8 %copy-start.2 = (bf16[384,640]{1,0:T(8,128)(2,1)S(1)}, bf16[384,640]{1,0:T(8,128)(2,1)}, u32[]{:S(2)}) copy-start(bf16[384,640]{1,0:T(8,128)(2,1)} %constant.49.clone.tables) | copy-start | bytes 1474564
  24.1 8.1 %collective-permute-start.5 = (f32[144,32,128]{2,1,0:T(8,128)S(1)}, f32[144,32,128]{2,1,0:T(8,128)S(1)}, u32[]{:S(2)}, u32[]{:S(2)}) collective-permute-start(f32[144,32,128]{2,1,0:T(8,128)S(1)} %get-tuple-element.36.own), channel_id=1, source_target_pairs={{0,1},{1,0},{2,3},{3,2},{4,5},{5,4},{6,7},{7,6},{8,9},{9,8},{10,11... | collective-permute-start | bytes 7077896 | tf_op jit(solution)/shard_map/ppermute | solution.py:816
  24.8 11.1 %collective-permute-start.6 = (f32[5,32,128]{2,1,0:T(8,128)S(1)}, f32[5,32,128]{2,1,0:T(8,128)S(1)}, u32[]{:S(2)}, u32[]{:S(2)}) collective-permute-start(f32[5,32,128]{2,1,0:T(8,128)S(1)} %get-tuple-element.39), channel_id=1, source_target_pairs={{0,2},{1,3},{2,4},{3,5},{4,6},{5,7},{6,8},{7,9},{8,10},{9,11},{10,... | collective-permute-start | bytes 245768 | tf_op jit(solution)/shard_map/ppermute | solution.py:816
  24.8 13.1 %copy-start = (f32[4,27,4096]{2,0,1:T(4,128)S(1)}, f32[4,27,4096]{2,0,1:T(4,128)}, u32[]{:S(2)}) copy-start(f32[4,27,4096]{2,0,1:T(4,128)} %param.11) | copy-start | bytes 5308420
  24.8 13.1 %copy-start.1 = (f32[4,9,4096]{2,0,1:T(4,128)S(1)}, f32[4,9,4096]{2,0,1:T(4,128)}, u32[]{:S(2)}) copy-start(f32[4,9,4096]{2,0,1:T(4,128)} %param.12) | copy-start | bytes 1769476
  24.8 13.1 %copy-start.3 = (bf16[128,640]{1,0:T(8,128)(2,1)S(1)}, bf16[128,640]{1,0:T(8,128)(2,1)}, u32[]{:S(2)}) copy-start(bf16[128,640]{1,0:T(8,128)(2,1)} %constant.50.clone.weights) | copy-start | bytes 491524
  24.8 11.1 %collective-permute-start.7 = (f32[5,32,128]{2,1,0:T(8,128)S(1)}, f32[5,32,128]{2,1,0:T(8,128)S(1)}, u32[]{:S(2)}, u32[]{:S(2)}) collective-permute-start(f32[5,32,128]{2,1,0:T(8,128)S(1)} %get-tuple-element.40), channel_id=1, source_target_pairs={{0,254},{1,255},{2,0},{3,1},{4,2},{5,3},{6,4},{7,5},{8,6},{9,7},{1... | collective-permute-start | bytes 245768 | tf_op jit(solution)/shard_map/ppermute | solution.py:816
  35.9 1.7 %collective-permute-start.8 = (f32[5,32,128]{2,1,0:T(8,128)S(1)}, f32[5,32,128]{2,1,0:T(8,128)S(1)}, u32[]{:S(2)}, u32[]{:S(2)}) collective-permute-start(f32[5,32,128]{2,1,0:T(8,128)S(1)} %collective-permute-done.6.up_own), channel_id=1, source_target_pairs={{0,1},{1,0},{2,3},{3,2},{4,5},{5,4},{6,7},{7,6},{8,9},{9,8},{10,11... | collective-permute-start | bytes 245768 | tf_op jit(solution)/shard_map/ppermute | solution.py:816
  36.7 1.3 %collective-permute-start.9 = (f32[5,32,128]{2,1,0:T(8,128)S(1)}, f32[5,32,128]{2,1,0:T(8,128)S(1)}, u32[]{:S(2)}, u32[]{:S(2)}) collective-permute-start(f32[5,32,128]{2,1,0:T(8,128)S(1)} %collective-permute-done.7.down_own), channel_id=1, source_target_pairs={{0,1},{1,0},{2,3},{3,2},{4,5},{5,4},{6,7},{7,6},{8,9},{9,8},{10,11... | collective-permute-start | bytes 245768 | tf_op jit(solution)/shard_map/ppermute | solution.py:816

commit v2 on v1

--- a/solution.py
+++ b/solution.py
@@ -194,10 +194,8 @@
 
 def pack_faces(out, up, down, meta=None):
     lane = iota(CHUNK, 1) % 16
-
-    @pl.loop(0, 4)
-    def _(v):
-        at = chunk_at(v)
+    for v in range(4):
+        at = pl.ds(8 * v, 8)
         for ref, digit, start in ((up, 2, 15), (down, 0, 0)):
             for b in range(4):
                 fields = [out[b * PER_BLOCK + 3 * e + digit, at, :] for e in range(9)]
@@ -855,7 +853,8 @@
         12,
         1 << 27,
     )(info, levels, diffusivity, stoichiometry, own, other)
-    held, up, down = lax.optimization_barrier((held, up, down))
+    held, up = lax.optimization_barrier((held, up))
+    held, down = lax.optimization_barrier((held, down))
     arrived = (up, move(up, swap), down, move(down, swap))
     landing = [vmem(2, 8), vmem(2, 8), vmem(2, 8), vmem(2, 2)]
     own_next, up_next, down_next, table = call(
@@ -887,7 +886,8 @@
         14,
         1 << 27,
     )(info, levels, near, diffusivity, stoichiometry, own_next, other_next, own, other, side_table)
-    held, sides, up, down = lax.optimization_barrier((held, sides, up, down))
+    held, sides, up = lax.optimization_barrier((held, sides, up))
+    held, sides, down = lax.optimization_barrier((held, sides, down))
     pop_out, scal_out, returned = call(
         end_kernel,
         "aaaaa" + "v" * 15,

time: 41.4 us -> 40.5 us (0.978); the launches traced: 41.5 us -> 41 us
  starting transfers between devices: 21.4 us -> 20.4 us
  Pallas kernels: 16.1 us -> 16.8 us
    ppermute x10, starting transfers between devices: 21.4 us -> 20.4 us  [move(): return lax.ppermute(x, 'blk', pairs)]
  transfers between devices with their start and end apart: 10 -> 10, of which waited for: 5 -> 5; matrix products, arithmetic and copies ran while one was open for 0% -> 0% of each run, Pallas kernels for 14% -> 15%
where the time goes in v2:
time: 40.5 us; the launch traced here: 41 us
  starting transfers between devices  20.4 us (50%)
  Pallas kernels  16.8 us (41%)
  waiting for transfers between devices  2.79 us (7%)
  between operations  0.82 us (2%)
    ppermute x10, starting transfers between devices, move(): return lax.ppermute(x, 'blk', pairs)  20.4 us
    pallas_call x1, Pallas kernels, local(): call(middle_kernel, 'aaaaavvvvvvv', [shape_of(fields, *full), shape_of(5,...  3.92 us
    pallas_call x1, Pallas kernels, local(): call(end_kernel, 'aaaaa' + 'v' * 15, [shape_of(27, 128, LANES), shape_of(...  3.81 us
    pallas_call x1, Pallas kernels, local(): call(second_plane_kernel, 'aaaaavvvvv', [shape_of(4, 27, *full), shape_of...  3.81 us
    pallas_call x1, Pallas kernels, local(): call(begin_kernel, 'ahhhhhhh', [shape_of(FIELDS, *full), shape_of(5, *ful...  2.93 us
    ppermute x10, waiting for transfers between devices, move(): return lax.ppermute(x, 'blk', pairs)  2.79 us
    pallas_call x1, Pallas kernels, local(): call(plane_kernel, 'aaaavv', [shape_of(4, 27, *full), table_shape, shape_...  2.37 us
  transfers between devices with their start and end apart: 10, of which 5 were waited for; matrix products, arithmetic and copies ran while one was open for 0% of the time, Pallas kernels for 15%

profile of v2, /device:TPU:1, one launch (start us, length us, event | category | flops | bytes accessed | tf_op | source)
XLA Modules:
  0.0 41.0 jit_solution(13896191444060793934)
XLA Ops:
  0.6 0.0 copy-start.4
  0.6 0.0 copy-start.5
  0.7 0.1 pad_add_fusion.info_in
  0.8 2.9 %begin.1 = (f32[145,32,128]{2,1,0:T(8,128)S(1)}, f32[5,32,128]{2,1,0:T(8,128)S(1)}, f32[5,32,128]{2,1,0:T(8,128)S(1)}) custom-call(s32[4]{0:T(128)S(1)} %pad_add_fusion.info_in, s32[1024]{0:T(1024)} %levels_in.9, s32[4,6]{1,0:T(4,128)} %near_in.1, f32[27]{0:T(128)} %rates_in.3, f32[27,128,128]{2,1,0:T(8,128)} %bitcast.34, f32[9,128,128]{2,1,0:T(8,128)} %bitcast.36, ...), custom_call_target="tpu_custom_call" | custom-call | flops 134217728 | bytes 8388608 | tf_op jit(solution)/shard_map/begin/pallas_call | solution.py:825
  3.7 3.3 %collective-permute-start = (f32[145,32,128]{2,1,0:T(8,128)S(1)}, f32[145,32,128]{2,1,0:T(8,128)S(1)}, u32[]{:S(2)}, u32[]{:S(2)}) collective-permute-start(f32[145,32,128]{2,1,0:T(8,128)S(1)} %get-tuple-element.29.own.own_before), channel_id=1, source_target_pairs={{0,1},{1,0},{2,3},{3,2},{4,5},{5,4},{6,7},{7,6},{8,9},{9,8},{10,11... | collective-permute-start | bytes 7127048 | tf_op jit(solution)/shard_map/ppermute | solution.py:814
  7.0 0.0 collective-permute-start.1
  7.0 8.5 %collective-permute-start.2 = (f32[5,32,128]{2,1,0:T(8,128)S(1)}, f32[5,32,128]{2,1,0:T(8,128)S(1)}, u32[]{:S(2)}, u32[]{:S(2)}) collective-permute-start(f32[5,32,128]{2,1,0:T(8,128)S(1)} %get-tuple-element.34), channel_id=1, source_target_pairs={{0,254},{1,255},{2,0},{3,1},{4,2},{5,3},{6,4},{7,5},{8,6},{9,7},{1... | collective-permute-start | bytes 245768 | tf_op jit(solution)/shard_map/ppermute | solution.py:814
  15.6 0.0 collective-permute-done.other.other_before
  15.6 2.4 %plane.1 = (f32[4,27,32,128]{3,2,1,0:T(8,128)S(1)}, s32[8,128]{1,0:T(8,128)S(1)}, f32[144,32,128]{2,1,0:T(8,128)S(1)}) custom-call(s32[4]{0:T(128)S(1)} %pad_add_fusion.info_in, s32[1024]{0:T(1024)S(1)} %copy-done.4, f32[9]{0:T(128)S(1)} %copy-done.5, f32[9]{0:T(128)S(1)} %copy-done.7, f32[145,32,128]{2,1,0:T(8,128)S(1)} %get-tuple-element.29.own.own_before, ...), custom_call_target="tpu_custom_call" | custom-call | flops 134217728 | bytes 8388608 | tf_op jit(solution)/shard_map/plane/pallas_call | solution.py:845
  17.9 0.3 collective-permute-done.1.up_own.up_own_before
  18.3 0.0 collective-permute-done.2.down_own.down_own_before
  18.3 0.7 %collective-permute-start.4 = (f32[5,32,128]{2,1,0:T(8,128)S(1)}, f32[5,32,128]{2,1,0:T(8,128)S(1)}, u32[]{:S(2)}, u32[]{:S(2)}) collective-permute-start(f32[5,32,128]{2,1,0:T(8,128)S(1)} %collective-permute-done.2.down_own.down_own_before), channel_id=1, source_target_pairs={{0,1},{1,0},{2,3},{3,2},{4,5},{5,4},{6,7},{7,6},{8,9},{9,8},{10,11... | collective-permute-start | bytes 245768 | tf_op jit(solution)/shard_map/ppermute | solution.py:814
  18.9 0.0 collective-permute-start.3
  18.9 0.9 %collective-permute-done.4.down_other.down_other_before = f32[5,32,128]{2,1,0:T(8,128)S(1)} collective-permute-done((f32[5,32,128]{2,1,0:T(8,128)S(1)}, f32[5,32,128]{2,1,0:T(8,128)S(1)}, u32[]{:S(2)}, u32[]{:S(2)}) %collective-permute-start.4) | collective-permute-done | bytes 81952 | tf_op jit(solution)/shard_map/ppermute | solution.py:814
  19.9 0.4 collective-permute-done.3.up_other.up_other_before
  20.2 0.0 copy-done.6
  20.2 3.9 %middle.1 = (f32[144,32,128]{2,1,0:T(8,128)S(1)}, f32[5,32,128]{2,1,0:T(8,128)S(1)}, f32[5,32,128]{2,1,0:T(8,128)S(1)}, s32[8,128]{1,0:T(8,128)S(1)}) custom-call(s32[4]{0:T(128)S(1)} %pad_add_fusion.info_in, s32[1024]{0:T(1024)S(1)} %copy-done.4, s32[8,128]{1,0:T(8,128)S(1)} %get-tuple-element.30.near_in, f32[27]{0:T(128)S(1)} %copy-done.6, ...), custom_call_target="tpu_custom_call" | custom-call | flops 268435456 | bytes 8388608 | tf_op jit(solution)/shard_map/middle/pallas_call | solution.py:860
  24.2 0.1 collective-permute-start.5
  24.3 0.1 collective-permute-start.6
  24.4 0.0 copy-start
  24.4 0.0 copy-start.1
  24.4 0.0 copy-start.3
  24.4 6.9 %collective-permute-start.7 = (f32[5,32,128]{2,1,0:T(8,128)S(1)}, f32[5,32,128]{2,1,0:T(8,128)S(1)}, u32[]{:S(2)}, u32[]{:S(2)}) collective-permute-start(f32[5,32,128]{2,1,0:T(8,128)S(1)} %get-tuple-element.46), channel_id=1, source_target_pairs={{0,254},{1,255},{2,0},{3,1},{4,2},{5,3},{6,4},{7,5},{8,6},{9,7},{1... | collective-permute-start | bytes 245768 | tf_op jit(solution)/shard_map/ppermute | solution.py:814
  31.2 0.0 collective-permute-done.5.other
  31.2 3.8 %plane2.1 = (f32[4,27,32,128]{3,2,1,0:T(8,128)S(1)}, f32[4,2304]{1,0:T(4,128)S(1)}, f32[144,32,128]{2,1,0:T(8,128)S(1)}) custom-call(s32[4]{0:T(128)S(1)} %pad_add_fusion.info_in, s32[1024]{0:T(1024)S(1)} %copy-done.4, s32[8,128]{1,0:T(8,128)S(1)} %get-tuple-element.30.near_in, f32[9]{0:T(128)S(1)} %copy-done.5, f32[9]{0:T(128)S(1)} %copy-done.7, ...), custom_call_target="tpu_custom_call" | custom-call | flops 134217728 | bytes 8388608 | tf_op jit(solution)/shard_map/plane2/pallas_call | solution.py:877
  35.1 0.0 collective-permute-done.6.up_own
  35.1 0.0 collective-permute-done.7.down_own
  35.1 0.8 %collective-permute-start.9 = (f32[5,32,128]{2,1,0:T(8,128)S(1)}, f32[5,32,128]{2,1,0:T(8,128)S(1)}, u32[]{:S(2)}, u32[]{:S(2)}) collective-permute-start(f32[5,32,128]{2,1,0:T(8,128)S(1)} %collective-permute-done.7.down_own), channel_id=1, source_target_pairs={{0,1},{1,0},{2,3},{3,2},{4,5},{5,4},{6,7},{7,6},{8,9},{9,8},{10,11... | collective-permute-start | bytes 245768 | tf_op jit(solution)/shard_map/ppermute | solution.py:814
  35.9 0.1 collective-permute-start.8
  36.0 0.8 %collective-permute-done.9.down_other = f32[5,32,128]{2,1,0:T(8,128)S(1)} collective-permute-done((f32[5,32,128]{2,1,0:T(8,128)S(1)}, f32[5,32,128]{2,1,0:T(8,128)S(1)}, u32[]{:S(2)}, u32[]{:S(2)}) %collective-permute-start.9) | collective-permute-done | bytes 81952 | tf_op jit(solution)/shard_map/ppermute | solution.py:814
  36.8 0.4 collective-permute-done.8.up_other
  37.2 3.8 %end.1 = (f32[27,128,128]{2,1,0:T(8,128)}, f32[9,128,128]{2,1,0:T(8,128)}, f32[4,3456]{1,0:T(4,128)}) custom-call(s32[4]{0:T(128)S(1)} %pad_add_fusion.info_in, s32[1024]{0:T(1024)S(1)} %copy-done.4, s32[8,128]{1,0:T(8,128)S(1)} %get-tuple-element.30.near_in, s32[8,128]{1,0:T(8,128)S(1)} %get-tuple-element.39.far_in, f32[9]{0:T(128)S(1)} %copy-done.5, ...), custom_call_target="tpu_custom_call" | custom-call | flops 134217728 | bytes 8388608 | tf_op jit(solution)/shard_map/end/pallas_call | solution.py:891
  (10 shorter events, 0.0 us)
Async XLA Ops:
  0.6 14.9 %copy-start.4 = (s32[1024]{0:T(1024)S(1)}, s32[1024]{0:T(1024)}, u32[]{:S(2)}) copy-start(s32[1024]{0:T(1024)} %levels_in.9) | copy-start | bytes 12292
  0.6 14.9 %copy-start.5 = (f32[9]{0:T(128)S(1)}, f32[9]{0:T(128)}, u32[]{:S(2)}) copy-start(f32[9]{0:T(128)} %diffusivity_in.7) | copy-start | bytes 112
  0.7 14.9 %copy-start.7 = (f32[9]{0:T(128)S(1)}, f32[9]{0:T(128)}, u32[]{:S(2)}) copy-start(f32[9]{0:T(128)} %stoichiometry_in.3) | copy-start | bytes 112
  3.7 11.8 %collective-permute-start = (f32[145,32,128]{2,1,0:T(8,128)S(1)}, f32[145,32,128]{2,1,0:T(8,128)S(1)}, u32[]{:S(2)}, u32[]{:S(2)}) collective-permute-start(f32[145,32,128]{2,1,0:T(8,128)S(1)} %get-tuple-element.29.own.own_before), channel_id=1, source_target_pairs={{0,1},{1,0},{2,3},{3,2},{4,5},{5,4},{6,7},{7,6},{8,9},{9,8},{10,11... | collective-permute-start | bytes 7127048 | tf_op jit(solution)/shard_map/ppermute | solution.py:814
  7.0 11.2 %collective-permute-start.1 = (f32[5,32,128]{2,1,0:T(8,128)S(1)}, f32[5,32,128]{2,1,0:T(8,128)S(1)}, u32[]{:S(2)}, u32[]{:S(2)}) collective-permute-start(f32[5,32,128]{2,1,0:T(8,128)S(1)} %get-tuple-element.32), channel_id=1, source_target_pairs={{0,2},{1,3},{2,4},{3,5},{4,6},{5,7},{6,8},{7,9},{8,10},{9,11},{10,... | collective-permute-start | bytes 245768 | tf_op jit(solution)/shard_map/ppermute | solution.py:814
  7.0 13.2 %copy-start.6 = (f32[27]{0:T(128)S(1)}, f32[27]{0:T(128)}, u32[]{:S(2)}) copy-start(f32[27]{0:T(128)} %rates_in.3) | copy-start | bytes 328
  7.0 11.2 %collective-permute-start.2 = (f32[5,32,128]{2,1,0:T(8,128)S(1)}, f32[5,32,128]{2,1,0:T(8,128)S(1)}, u32[]{:S(2)}, u32[]{:S(2)}) collective-permute-start(f32[5,32,128]{2,1,0:T(8,128)S(1)} %get-tuple-element.34), channel_id=1, source_target_pairs={{0,254},{1,255},{2,0},{3,1},{4,2},{5,3},{6,4},{7,5},{8,6},{9,7},{1... | collective-permute-start | bytes 245768 | tf_op jit(solution)/shard_map/ppermute | solution.py:814
  18.3 1.6 %collective-permute-start.4 = (f32[5,32,128]{2,1,0:T(8,128)S(1)}, f32[5,32,128]{2,1,0:T(8,128)S(1)}, u32[]{:S(2)}, u32[]{:S(2)}) collective-permute-start(f32[5,32,128]{2,1,0:T(8,128)S(1)} %collective-permute-done.2.down_own.down_own_before), channel_id=1, source_target_pairs={{0,1},{1,0},{2,3},{3,2},{4,5},{5,4},{6,7},{7,6},{8,9},{9,8},{10,11... | collective-permute-start | bytes 245768 | tf_op jit(solution)/shard_map/ppermute | solution.py:814
  18.9 1.3 %collective-permute-start.3 = (f32[5,32,128]{2,1,0:T(8,128)S(1)}, f32[5,32,128]{2,1,0:T(8,128)S(1)}, u32[]{:S(2)}, u32[]{:S(2)}) collective-permute-start(f32[5,32,128]{2,1,0:T(8,128)S(1)} %collective-permute-done.1.up_own.up_own_before), channel_id=1, source_target_pairs={{0,1},{1,0},{2,3},{3,2},{4,5},{5,4},{6,7},{7,6},{8,9},{9,8},{10,11... | collective-permute-start | bytes 245768 | tf_op jit(solution)/shard_map/ppermute | solution.py:814
  20.2 11.0 %copy-start.2 = (bf16[384,640]{1,0:T(8,128)(2,1)S(1)}, bf16[384,640]{1,0:T(8,128)(2,1)}, u32[]{:S(2)}) copy-start(bf16[384,640]{1,0:T(8,128)(2,1)} %constant.49.clone.tables) | copy-start | bytes 1474564
  24.2 7.1 %collective-permute-start.5 = (f32[144,32,128]{2,1,0:T(8,128)S(1)}, f32[144,32,128]{2,1,0:T(8,128)S(1)}, u32[]{:S(2)}, u32[]{:S(2)}) collective-permute-start(f32[144,32,128]{2,1,0:T(8,128)S(1)} %get-tuple-element.40.own), channel_id=1, source_target_pairs={{0,1},{1,0},{2,3},{3,2},{4,5},{5,4},{6,7},{7,6},{8,9},{9,8},{10,11... | collective-permute-start | bytes 7077896 | tf_op jit(solution)/shard_map/ppermute | solution.py:814
  24.3 10.8 %collective-permute-start.6 = (f32[5,32,128]{2,1,0:T(8,128)S(1)}, f32[5,32,128]{2,1,0:T(8,128)S(1)}, u32[]{:S(2)}, u32[]{:S(2)}) collective-permute-start(f32[5,32,128]{2,1,0:T(8,128)S(1)} %get-tuple-element.43), channel_id=1, source_target_pairs={{0,2},{1,3},{2,4},{3,5},{4,6},{5,7},{6,8},{7,9},{8,10},{9,11},{10,... | collective-permute-start | bytes 245768 | tf_op jit(solution)/shard_map/ppermute | solution.py:814
  24.4 12.8 %copy-start = (f32[4,27,4096]{2,0,1:T(4,128)S(1)}, f32[4,27,4096]{2,0,1:T(4,128)}, u32[]{:S(2)}) copy-start(f32[4,27,4096]{2,0,1:T(4,128)} %param.11) | copy-start | bytes 5308420
  24.4 12.8 %copy-start.1 = (f32[4,9,4096]{2,0,1:T(4,128)S(1)}, f32[4,9,4096]{2,0,1:T(4,128)}, u32[]{:S(2)}) copy-start(f32[4,9,4096]{2,0,1:T(4,128)} %param.12) | copy-start | bytes 1769476
  24.4 12.8 %copy-start.3 = (bf16[128,640]{1,0:T(8,128)(2,1)S(1)}, bf16[128,640]{1,0:T(8,128)(2,1)}, u32[]{:S(2)}) copy-start(bf16[128,640]{1,0:T(8,128)(2,1)} %constant.50.clone.weights) | copy-start | bytes 491524
  24.4 10.7 %collective-permute-start.7 = (f32[5,32,128]{2,1,0:T(8,128)S(1)}, f32[5,32,128]{2,1,0:T(8,128)S(1)}, u32[]{:S(2)}, u32[]{:S(2)}) collective-permute-start(f32[5,32,128]{2,1,0:T(8,128)S(1)} %get-tuple-element.46), channel_id=1, source_target_pairs={{0,254},{1,255},{2,0},{3,1},{4,2},{5,3},{6,4},{7,5},{8,6},{9,7},{1... | collective-permute-start | bytes 245768 | tf_op jit(solution)/shard_map/ppermute | solution.py:814
  35.1 1.7 %collective-permute-start.9 = (f32[5,32,128]{2,1,0:T(8,128)S(1)}, f32[5,32,128]{2,1,0:T(8,128)S(1)}, u32[]{:S(2)}, u32[]{:S(2)}) collective-permute-start(f32[5,32,128]{2,1,0:T(8,128)S(1)} %collective-permute-done.7.down_own), channel_id=1, source_target_pairs={{0,1},{1,0},{2,3},{3,2},{4,5},{5,4},{6,7},{7,6},{8,9},{9,8},{10,11... | collective-permute-start | bytes 245768 | tf_op jit(solution)/shard_map/ppermute | solution.py:814
  35.9 1.3 %collective-permute-start.8 = (f32[5,32,128]{2,1,0:T(8,128)S(1)}, f32[5,32,128]{2,1,0:T(8,128)S(1)}, u32[]{:S(2)}, u32[]{:S(2)}) collective-permute-start(f32[5,32,128]{2,1,0:T(8,128)S(1)} %collective-permute-done.6.up_own), channel_id=1, source_target_pairs={{0,1},{1,0},{2,3},{3,2},{4,5},{5,4},{6,7},{7,6},{8,9},{9,8},{10,11... | collective-permute-start | bytes 245768 | tf_op jit(solution)/shard_map/ppermute | solution.py:814
